TPU v7x, 128 devices: a whole 4x4x4 slice. The times are simulated.
128 devices in a mesh: row: 8 (over x_hi, y), col: 16 (over z, x_lo, core).
Axes of the slice: x: 4 (x_hi: 2, x_lo: 2; x = x_hi * 2 + x_lo), y: 4, z: 4, core: 2. Of those that a mesh axis runs over, the one named last changes fastest.
Arguments:
- velocity: float32 [3, 16, 16, 36, 32, 512], P(None, 'col', 'row'), may hold values from -6 to 6
- y_sizes: int32 [16], replicated, may hold values from 1 to 36, 512 in all
- old_place: int32 [16, 16], replicated, may hold values from 0 to 15, each once within a row
- new_col: int32 [16, 16], replicated, may hold values from 0 to 15, each once within a row
Outputs:
- divergence: float32 [16, 16, 2, 512, 512], P('row', 'col')
- peak: float32 [512, 512], replicated
Inputs may be any that keep to these rules, and one draw needn't show every extreme that they name: `y_sizes`: the heights sum to 512 and the tallest is exactly 36. `old_place`: each row is a permutation of 0 to 15. `new_col`: each row is a permutation of 0 to 16 - 1.
All inputs are finite; a program needn't handle non-finite values.
Results may differ from a plain program's by a relative error of at most 0.0003.
Values sent between devices are 32-bit elements; how exact they have to be, the bound alone decides.
No kernel may reach another device: no remote copies, remote signals or barrier semaphores. Data moves between devices by JAX's collectives and lax.ppermute only.
A program may use at most 320 MiB of HBM per device.

v0:
```python
import math

import jax
import jax.numpy as jnp
from jax import lax
from jax.sharding import PartitionSpec as P

YMEAN = 32


EXACT = lax.Precision.HIGHEST


def items_in_groups(array, axis, split_dim, concat_dim, work, item_dim, out_dim):

    def moved(group):
        return lax.all_to_all(group, axis, split_axis=split_dim, concat_axis=concat_dim, tiled=True)

    items = jax.tree.leaves(array)[0].shape[item_dim]
    ends = [items * k // 2 for k in range(2 + 1)] if items % 2 == 0 else [0, items]
    groups = [
        jax.tree.map(lambda a: lax.slice_in_dim(a, low, high, axis=item_dim), array)
        for low, high in zip(ends, ends[1:])
    ]
    arrived = [moved(group) for group in groups]
    made = [work(group) for group in arrived]
    return jax.tree.map(lambda *parts: jnp.concatenate(parts, axis=out_dim), *made)


def source_rows(y_sizes, old_place, row_depth, height):
    ends = jnp.cumsum(y_sizes)
    starts = ends - y_sizes
    cells = jnp.arange(height, dtype=jnp.int32)
    block = jnp.sum((cells[:, None] >= ends[None, :]).astype(jnp.int32), axis=1)
    offset = cells - jnp.take(starts, block)
    return jnp.take(old_place, block, axis=1) * row_depth + offset


def spectral_matrix(positions, count):
    gap = (positions[:, None] - positions[None, :]) % count
    angle = gap.astype(jnp.float32) * (math.pi / count)
    parity = 1.0 - 2.0 * (gap % 2).astype(jnp.float32)
    divisor = jnp.where(gap == 0, 1.0, jnp.sin(angle))
    return jnp.where(gap == 0, 0.0, parity * jnp.cos(angle) / divisor * (2.0 / count))


def along_last(field, matrix):
    return jnp.dot(
        field, jnp.transpose(matrix), precision=EXACT, preferred_element_type=jnp.float32
    )


def along_rows(field, matrix):
    return jnp.einsum("jy,ksyx->ksjx", matrix, field, precision=EXACT)


def vertical_positions(slab_of, rows_count, columns, per_row, planes, thick):
    owner_row = jnp.arange(rows_count, dtype=jnp.int32)[:, None, None]
    owner_col = jnp.arange(columns, dtype=jnp.int32)[None, :, None]
    group = jnp.arange(per_row, dtype=jnp.int32)[None, None, :]
    zblock = owner_row * per_row + group
    slab = jnp.take(slab_of.reshape(-1), zblock * columns + owner_col)
    first = zblock * planes + slab * thick
    return (first[..., None] + jnp.arange(thick, dtype=jnp.int32)).reshape(-1)


def on_device(velocity, y_sizes, old_place, new_col):
    velocity = velocity[:, 0]
    row_depth = velocity.shape[2]
    planes = velocity.shape[3]
    x_cells = velocity.shape[4]
    places = velocity.shape[1]
    columns = lax.axis_size("col")
    rows_count = lax.axis_size("row")
    my_col = lax.axis_index("col")
    my_row = lax.axis_index("row")
    thick = planes // columns
    per_row = columns // rows_count
    blocks_y = y_sizes.shape[0]
    height = YMEAN * blocks_y
    hits = (new_col[:, :, None] == jnp.arange(columns, dtype=jnp.int32)[None, None, :]).astype(
        jnp.int32
    )
    slab_of = jnp.sum(hits * jnp.arange(columns, dtype=jnp.int32)[None, :, None], axis=1)
    rows_index = source_rows(y_sizes, old_place, row_depth, height)
    across_x = spectral_matrix(jnp.arange(x_cells, dtype=jnp.int32), x_cells)
    across_y = spectral_matrix(jnp.arange(height, dtype=jnp.int32), height)
    fields = velocity.shape[0]
    order = jnp.take(slab_of, my_col, axis=0)
    sliced = velocity.reshape(fields, places, row_depth, columns, thick, x_cells)
    outgoing = jnp.take(sliced, order, axis=3)
    settled = lax.all_to_all(
        lax.all_to_all(outgoing, "col", split_axis=3, concat_axis=3, tiled=True),
        "row",
        split_axis=3,
        concat_axis=1,
        tiled=True,
    )
    flat = settled.reshape(fields, blocks_y * row_depth, per_row, thick, x_cells)
    my_rows = lax.dynamic_slice_in_dim(rows_index, my_row * per_row, per_row, 0)
    pieces = []
    for group in range(per_row):
        picked = jnp.take(flat[:, :, group], my_rows[group], axis=1)
        pieces.append(jnp.swapaxes(picked, 1, 2))
    slabs = jnp.stack(pieces, axis=1)
    vertical = slabs[2]
    positions = vertical_positions(slab_of, rows_count, columns, per_row, planes, thick)
    across_z = spectral_matrix(positions, planes * columns)

    def turn(received):
        shape = received.shape
        slope = jnp.einsum(
            "ab,byx->ayx", across_z, received.reshape(-1, shape[3], shape[4]), precision=EXACT
        )
        return lax.all_to_all(
            slope.reshape(shape), ("row", "col"), split_axis=0, concat_axis=3, tiled=True
        )

    slope_z = items_in_groups(vertical[None], ("row", "col"), 3, 0, turn, 4, 4)[0]
    slope_x = along_last(slabs[0], across_x)
    field = slope_x + along_rows(slabs[1], across_y) + slope_z
    local_peak = jnp.max(jnp.abs(field), axis=(0, 1))
    peak = lax.pmax(local_peak, ("row", "col"))
    return (field[:, None], peak)


def solution(mesh):
    in_specs = (P(None, "col", "row", None, None, None), P(), P(), P())
    out_specs = (P("row", "col", None, None, None), P())
    return jax.shard_map(
        on_device, mesh=mesh, in_specs=in_specs, out_specs=out_specs, check_vma=False
    )
```

profile of v0, /device:TPU:0, one launch (start us, length us, event | category | flops | bytes accessed | tf_op | source)
XLA Modules:
  0.0 785.8 jit_solution(15811812712693186008)
XLA Ops:
  8.0 16.8 %reshape_squeeze.3 = f32[3,2,36,16,2,512]{5,4,3,2,1,0:T(2,128)} reshape(f32[3,1,2,36,32,512]{5,4,3,2,1,0:T(8,128)} %param.6) | data formatting | bytes 28311552 | tf_op jit(solution)/shard_map/reshape;squeeze | solution.py:90
  24.8 28.0 %gather_fusion = f32[16,3,2,36,2,512]{5,4,3,2,1,0:T(2,128)} fusion(f32[3,2,36,16,2,512]{5,4,3,2,1,0:T(2,128)} %reshape_squeeze.3, s32[1024]{0:T(1024)S(1)} %pad_clamp_fusion.3), kind=kCustom, calls=%fused_computation.2 | custom fusion | bytes 28311616 | tf_op jit(solution)/shard_map/jit(_take)/gather | solution.py:91
  52.9 9.4 %select_bitcast_fusion = f32[3,2,36,16,2,512]{5,4,2,1,0,3:T(2,128)S(1)} fusion(f32[16,3,2,36,2,512]{5,4,3,2,1,0:T(2,128)} %gather_fusion, pred[16]{0:T(512)(128)(4,1)S(1)} %compare_and_fusion.3), kind=kLoop, calls=%fused_computation.11 | loop fusion | flops 3538944 | bytes 28311568 | tf_op jit(solution)/shard_map/jit(_take)/select_n | solution.py:91
  62.3 163.2 %all_to_all.86 = f32[3,2,36,16,2,512]{5,4,2,1,0,3:T(2,128)} all-to-all(f32[3,2,36,16,2,512]{5,4,2,1,0,3:T(2,128)S(1)} %select_bitcast_fusion), channel_id=1, replica_groups=mesh['row'=8,'col'=16] {'col'}, dimensions={3} | all-to-all | bytes 28311552 | tf_op jit(solution)/shard_map/all_to_all | solution.py:93
  225.5 7.0 all-to-all-start.1
  234.7 10.1 %fusion.60 = (s32[512]{0:T(512)S(1)}, pred[512]{0:T(512)(128)(4,1)S(1)}) fusion(s32[512]{0:T(512)S(1)} %bitcast.145, s32[]{:T(128)} %bitcast.3, s32[]{:T(128)} %bitcast.4, s32[]{:T(128)} %bitcast.5, s32[]{:T(128)} %bitcast.6, s32[]{:T(128)} %bitcast.7, s32[]{:T(128)} %bitcast.8, s32[]{:T(128)} %bitcast.9, s32[]{:T(128)} %bitcast.10, s32[]{:T(128)} %bitcast.11, ...), kind=kLoop, calls=%fused_computation.115 | loop fusion | flops 19456 | bytes 6720 | tf_op jit(solution)/shard_map/sub | solution.py:35
  245.5 142.1 %all-to-all-done.1 = f32[3,2,36,16,2,512]{5,4,2,1,0,3:T(2,128)} async-done(((f32[3,2,36,16,2,512]{5,4,2,1,0,3:T(2,128)}), f32[3,2,36,16,2,512]{5,4,2,1,0,3:T(2,128)}, u32[]{:S(2)}, u32[]{:S(2)}) %all-to-all-start.1) | async-done | bytes 14155808 | tf_op jit(solution)/shard_map/all_to_all | solution.py:92
  387.6 8.2 %copy.85 = f32[3,8,2,36,2,2,512]{6,5,4,3,2,1,0:T(2,128)S(1)} copy(f32[3,8,2,36,2,2,512]{6,5,3,2,0,4,1:T(2,128)} %bitcast.26) | data formatting | bytes 28311552 | tf_op jit(solution)/shard_map/all_to_all | solution.py:92
  395.8 8.2 %slice_bitcast_fusion.1 = (f32[3,576,2,512]{3,2,1,0:T(2,128)}, f32[3,576,2,512]{3,2,1,0:T(2,128)}) fusion(f32[3,576,2,2,512]{4,3,2,1,0:T(2,128)S(1)} %bitcast.136), kind=kLoop, calls=%fused_computation.13 | loop fusion | bytes 28311552 | tf_op jit(solution)/shard_map/squeeze | solution.py:103
  404.0 19.8 %gather_fusion.3 = f32[512,3,2,512]{3,2,1,0:T(2,128)} fusion(f32[3,576,2,512]{3,2,1,0:T(2,128)} %get-tuple-element.30, s32[1024]{0:T(1024)S(1)} %pad_clamp_fusion.2), kind=kCustom, calls=%fused_computation.clone | custom fusion | bytes 12584960 | tf_op jit(solution)/shard_map/jit(_take)/gather | solution.py:103
  423.8 7.1 fusion.1
  431.0 20.3 %gather_fusion.4 = f32[512,3,2,512]{3,2,1,0:T(2,128)} fusion(f32[3,576,2,512]{3,2,1,0:T(2,128)} %get-tuple-element.31, s32[1024]{0:T(1024)S(1)} %pad_clamp_fusion.1), kind=kCustom, calls=%fused_computation.1.clone | custom fusion | bytes 12584960 | tf_op jit(solution)/shard_map/jit(_take)/gather | solution.py:103
  462.1 6.9 all-to-all-start.4
  473.5 25.9 %all-to-all-done.4 = f32[1,2,2,512,256]{4,2,1,0,3:T(2,128)S(1)} async-done(((f32[1,2,2,512,256]{4,2,1,0,3:T(2,128)}), f32[1,2,2,512,256]{4,2,1,0,3:T(2,128)S(1)}, u32[]{:S(2)}, u32[]{:S(2)}) %all-to-all-start.4) | async-done | bytes 2097184 | tf_op jit(solution)/shard_map/all_to_all | solution.py:17
  515.9 10.0 %fusion.14 = f32[128,2,2,4,256]{4,0,3,2,1:T(8,128)S(1)} fusion(f32[512,4,256,1,1]{2,0,1,3,4:T(8,128)} %reshape.388, s32[512]{0:T(512)S(1)} %add.321, s32[128,2,2]{0,2,1:T(2,128)S(1)} %iota_add_fusion.2), kind=kOutput, calls=%fused_computation.30 | convolution fusion | flops 3230138368 | bytes 4198400 | tf_op jit(solution)/shard_map/ab,byx->ayx/dot_general | solution.py:112
  528.6 7.2 all-to-all-done.2
  535.8 6.2 all-to-all-start.5
  546.7 8.4 %fusion.16 = f32[128,2,2,4,256]{4,0,3,2,1:T(8,128)S(1)} fusion(f32[512,4,256,1,1]{2,0,1,3,4:T(8,128)S(1)} %reshape.387, s32[512]{0:T(512)S(1)} %add.321, s32[128,2,2]{0,2,1:T(2,128)S(1)} %iota_add_fusion.2), kind=kOutput, calls=%fused_computation.32 | convolution fusion | flops 3230138368 | bytes 4198400 | tf_op jit(solution)/shard_map/ab,byx->ayx/dot_general | solution.py:112
  557.8 14.1 %all-to-all-done.5 = f32[128,2,2,4,256]{4,3,2,1,0:T(4,128)} async-done(((f32[128,2,2,4,256]{4,3,2,1,0:T(4,128)}), f32[128,2,2,4,256]{4,3,2,1,0:T(4,128)}, u32[]{:S(2)}, u32[]{:S(2)}) %all-to-all-start.5) | async-done | bytes 2097184 | tf_op jit(solution)/shard_map/all_to_all | solution.py:115
  571.9 4.6 all-to-all-start.3
  576.8 15.6 %fusion.4 = f32[2,2,512,512]{3,2,1,0:T(8,128)} fusion(f32[3,1,2,512,512]{4,3,2,1,0:T(8,128)} %fusion.1, f32[3,1,2,512,512]{4,3,2,1,0:T(8,128)} %copy-done), kind=kOutput, calls=%fused_computation.20 | convolution fusion | flops 6452412416 | bytes 16777216 | tf_op jit(solution)/shard_map/dot_general | solution.py:48
  598.6 8.4 %all-to-all-done.3 = f32[128,2,2,4,256]{4,3,2,1,0:T(4,128)S(1)} async-done(((f32[128,2,2,4,256]{4,3,2,1,0:T(4,128)}), f32[128,2,2,4,256]{4,3,2,1,0:T(4,128)S(1)}, u32[]{:S(2)}, u32[]{:S(2)}) %all-to-all-start.3) | async-done | bytes 2097184 | tf_op jit(solution)/shard_map/all_to_all | solution.py:115
  612.0 20.6 %abs_reduce_fusion = (f32[512,512]{1,0:T(8,128)}, f32[2,2,512,512]{3,2,1,0:T(8,128)}) fusion(f32[1,2,2,512,256]{4,3,2,1,0:T(8,128)S(1)} %copy-done.2, f32[1,2,2,512,256]{4,3,2,1,0:T(8,128)} %all_to_all.72, f32[2,2,512,512]{3,2,1,0:T(8,128)} %fusion.4, f32[3,1,2,512,512]{4,3,2,1,0:T(8,128)} %fusion.1, f32[3,1,2,512,512]{4,3,2,1,0:T(8,128)} %copy-done), kind=kOutput, calls=%fused_computation.27 | convolution fusion | flops 6457393152 | bytes 26214400 | tf_op jit(solution)/shard_map/jy,ksyx->ksjx/dot_general | solution.py:54
  632.6 143.9 %all-reduce.2.cloned.1.call-done = f32[512,512]{1,0:T(8,128)} async-done(((f32[512,512]{1,0:T(8,128)}), f32[512,512]{1,0:T(8,128)}) %all-reduce.2.cloned.1.call-update) | async-done | bytes 1048592 | tf_op jit(solution)/shard_map/pmax | solution.py:123
  (70 shorter events, 59.2 us)
Async XLA Ops:
  225.5 7.0 copy-start.3
  225.5 7.1 copy-start.4
  225.5 162.1 %all-to-all-start.1 = ((f32[3,2,36,16,2,512]{5,4,2,1,0,3:T(2,128)}), f32[3,2,36,16,2,512]{5,4,2,1,0,3:T(2,128)}, u32[]{:S(2)}, u32[]{:S(2)}) async-start(f32[3,2,36,16,2,512]{5,4,2,1,0,3:T(2,128)} %all_to_all.86), calls=%async_computation.1 | async-start | bytes 28311552 | tf_op jit(solution)/shard_map/all_to_all | solution.py:92
  451.2 4.6 slice-start
  451.2 4.7 slice-start.1
  455.9 3.3 copy-start
  462.1 37.3 %all-to-all-start.4 = ((f32[1,2,2,512,256]{4,2,1,0,3:T(2,128)}), f32[1,2,2,512,256]{4,2,1,0,3:T(2,128)S(1)}, u32[]{:S(2)}, u32[]{:S(2)}) async-start(f32[1,2,2,512,256]{4,2,1,0,3:T(2,128)} %copy.97), calls=%async_computation.4 | async-start | bytes 4194304 | tf_op jit(solution)/shard_map/all_to_all | solution.py:17
  499.4 1.3 copy-start.1
  500.7 35.1 %all-to-all-start.2 = ((f32[1,2,2,512,256]{4,2,1,0,3:T(2,128)}), f32[1,2,2,512,256]{4,2,1,0,3:T(2,128)S(1)}, u32[]{:S(2)}, u32[]{:S(2)}) async-start(f32[1,2,2,512,256]{4,2,1,0,3:T(2,128)} %copy.93), calls=%async_computation.2 | async-start | bytes 4194304 | tf_op jit(solution)/shard_map/all_to_all | solution.py:17
  535.8 36.2 %all-to-all-start.5 = ((f32[128,2,2,4,256]{4,3,2,1,0:T(4,128)}), f32[128,2,2,4,256]{4,3,2,1,0:T(4,128)}, u32[]{:S(2)}, u32[]{:S(2)}) async-start(f32[128,2,2,4,256]{4,3,2,1,0:T(4,128)} %copy.99), calls=%async_computation.5 | async-start | bytes 4194304 | tf_op jit(solution)/shard_map/all_to_all | solution.py:115
  571.9 35.1 %all-to-all-start.3 = ((f32[128,2,2,4,256]{4,3,2,1,0:T(4,128)}), f32[128,2,2,4,256]{4,3,2,1,0:T(4,128)S(1)}, u32[]{:S(2)}, u32[]{:S(2)}) async-start(f32[128,2,2,4,256]{4,3,2,1,0:T(4,128)} %copy.95), calls=%async_computation.3 | async-start | bytes 4194304 | tf_op jit(solution)/shard_map/all_to_all | solution.py:115
  576.6 199.9 %all-reduce.2.cloned.1.call-start = ((), (), s32[]{:S(2)}) async-start(), calls=%async_computation.6 | async-start | bytes 2097152 | tf_op jit(solution)/shard_map/pmax | solution.py:123
  608.7 3.3 copy-start.2
Sparse Core Ops, SparseCore 0:
  632.8 143.6 all-reduce.1
where the time goes:
time: 794 us; the launch traced here: 786 us
  waiting for transfers between devices  342 us (43%)
  blocking collectives  163 us (21%)
  local copies, waits for them, and re-layouts  147 us (19%)
  matrix products  54.7 us (7%)
  other arithmetic  35 us (4%)
  starting transfers between devices  29.6 us (4%)
  between operations  14.6 us (2%)
    all_to_all x1, blocking collectives, on_device(): lax.all_to_all(outgoing, 'col', split_axis=3, concat_axis=3, tiled=True)  163 us
    pmax x1, waiting for transfers between devices, on_device(): peak = lax.pmax(local_peak, ('row', 'col'))  144 us
    all_to_all x1, waiting for transfers between devices, on_device(): lax.all_to_all(lax.all_to_all(outgoing, 'col', split_axis=3, concat_axis=...  142 us
    gather x2, local copies, waits for them, and re-layouts, on_device(): picked = jnp.take(flat[:, :, group], my_rows[group], axis=1)  40.1 us
    all_to_all x2, waiting for transfers between devices, moved(): lax.all_to_all(group, axis, split_axis=split_dim, concat_axis=concat_dim,...  33.1 us
    gather x1, local copies, waits for them, and re-layouts, on_device(): outgoing = jnp.take(sliced, order, axis=3)  28 us
    all_to_all x2, waiting for transfers between devices, turn(): lax.all_to_all(slope.reshape(shape), ('row', 'col'), split_axis=0, concat...  22.5 us
    dot_general x1, matrix products, along_rows(): return jnp.einsum('jy,ksyx->ksjx', matrix, field, precision=EXACT)  20.6 us
  transfers between devices with their start and end apart: 6, of which 6 were waited for; matrix products, arithmetic and copies ran while one was open for 10% of the time, Pallas kernels for 0%

commit v1 on v0

v1 whole, which is shorter than its diff:
```python
import jax
import jax.numpy as jnp
import numpy as np
from jax import lax
from jax.experimental import pallas as pl
from jax.experimental.pallas import tpu as pltpu
from jax.sharding import PartitionSpec as P

AXES = ("row", "col")
LANES = 128
N = 512
DEVICES = 128
KX = N // DEVICES
ROWS = 72
CAP = 36
ZB = 32
NB = 16
NR = 8


def spectral_pair():
    gap = (np.arange(N)[:, None] - np.arange(N)[None, :]) % N
    angle = gap * (np.pi / N)
    parity = 1.0 - 2.0 * (gap % 2)
    safe = np.where(gap == 0, 1.0, np.sin(angle))
    full = np.where(gap == 0, 0.0, parity * np.cos(angle) / safe * (2.0 / N))
    full = (full - full.T) / 2
    high = full.astype(jnp.bfloat16)
    low = (full - high.astype(np.float64)).astype(jnp.bfloat16)
    return high, low


def halves(value):
    high = value.astype(jnp.bfloat16)
    return high, (value - high.astype(jnp.float32)).astype(jnp.bfloat16)


def mul(left, right):
    return jnp.dot(left, right, preferred_element_type=jnp.float32)


def mul3(left, right):
    return mul(left[0], right[0]) + (mul(left[1], right[0]) + mul(left[0], right[1]))


def pack_rows(value, out_ref, i):
    tall = jnp.concatenate([value[:, k * LANES : (k + 1) * LANES] for k in range(KX)], axis=0)
    out_ref[:, i, :] = tall.T


def pack_plain(in_ref, out_ref):
    for i in range(8):
        pack_rows(in_ref[0, i], out_ref, i)


def pack_slope(in_ref, high_ref, low_ref, out_ref):
    flat = in_ref[0].reshape(8 * ZB, N)
    slope = -mul3(halves(flat), (high_ref[...], low_ref[...]))
    for i in range(8):
        pack_rows(slope[i * ZB : (i + 1) * ZB], out_ref, i)


def pack(velocity, field, matrices=None):
    specs = [pl.BlockSpec((1, 8, ZB, N), lambda t: (field, t, 0, 0))]
    args = [velocity]
    if matrices is not None:
        specs += [pl.BlockSpec((N, N), lambda t: (0, 0))] * 2
        args += list(matrices)
    return pl.pallas_call(
        pack_plain if matrices is None else pack_slope,
        grid=(ROWS // 8,),
        in_specs=specs,
        out_specs=pl.BlockSpec((DEVICES, 8, LANES), lambda t: (0, t, 0)),
        out_shape=jax.ShapeDtypeStruct((DEVICES, ROWS, LANES), jnp.float32),
        name="pack_slope" if matrices is not None else f"pack_{field}",
        cost_estimate=pl.CostEstimate(
            flops=2 * ROWS * ZB * N * N * (6 if matrices is not None else 1),
            bytes_accessed=2 * ROWS * ZB * N * 4,
            transcendentals=0,
        ),
    )(*args)


def gather_quad(starts, places, in_ref, lined, quad):
    for cc in range(4):
        for b in range(NB):
            place = places[quad * 4 + cc, b]
            source = in_ref[place // 2, cc, pl.ds((place % 2) * CAP, CAP), :]
            lined[cc, pl.ds(starts[b], CAP), :] = source


def turn_lanes(parts):
    lane = lax.broadcasted_iota(jnp.int32, parts[0].shape, 1)
    upper = (lane // 64) == 1
    odd = (lane // 32) % 2 == 1
    a0, a1, a2, a3 = parts
    b0 = jnp.where(upper, pltpu.roll(a2, 64, 1), a0)
    b2 = jnp.where(upper, a2, pltpu.roll(a0, 64, 1))
    b1 = jnp.where(upper, pltpu.roll(a3, 64, 1), a1)
    b3 = jnp.where(upper, a3, pltpu.roll(a1, 64, 1))
    c0 = jnp.where(odd, pltpu.roll(b1, 32, 1), b0)
    c1 = jnp.where(odd, b1, pltpu.roll(b0, 96, 1))
    c2 = jnp.where(odd, pltpu.roll(b3, 32, 1), b2)
    c3 = jnp.where(odd, b3, pltpu.roll(b2, 96, 1))
    return c0, c1, c2, c3


CHUNK = 64


def gather_kernel(starts, places, in_ref, out_ref, lined):
    gather_quad(starts, places, in_ref, lined, pl.program_id(0))

    def step(t, carry):
        rows = pl.ds(pl.multiple_of(t * CHUNK, CHUNK), CHUNK)
        turned = turn_lanes([lined[cc, rows, :] for cc in range(4)])
        for k in range(KX):
            out_ref[k, rows, :] = turned[k]
        return carry

    lax.fori_loop(0, N // CHUNK, step, 0)


LINED = 560


def gather(received, starts, places, name):
    return pl.pallas_call(
        gather_kernel,
        grid_spec=pltpu.PrefetchScalarGridSpec(
            num_scalar_prefetch=2,
            grid=(4,),
            in_specs=[pl.BlockSpec((NR, 4, ROWS, LANES), lambda q, *_: (0, q, 0, 0))],
            out_specs=pl.BlockSpec((KX, N, LANES), lambda q, *_: (0, 0, q)),
            scratch_shapes=[pltpu.VMEM((4, LINED, LANES), jnp.float32)],
        ),
        out_shape=jax.ShapeDtypeStruct((KX, N, N), jnp.float32),
        name=name,
        cost_estimate=pl.CostEstimate(
            flops=2 * N * N * N * 4, bytes_accessed=2 * KX * N * N * 4, transcendentals=0
        ),
    )(starts, places, received.reshape(NR, NB, ROWS, LANES))


def slope_z_kernel(field_ref, high_ref, low_ref, out_ref):
    out_ref[0] = -mul3(halves(field_ref[0]), (high_ref[...], low_ref[...]))


def slope_y_kernel(field_ref, high_ref, low_ref, add_ref, out_ref):
    out_ref[0] = add_ref[0] + mul3((high_ref[...], low_ref[...]), halves(field_ref[0]))


def slopes(kernel, field, matrices, extra, name):
    block = pl.BlockSpec((1, N, N), lambda k: (k, 0, 0))
    whole = pl.BlockSpec((N, N), lambda k: (0, 0))
    return pl.pallas_call(
        kernel,
        grid=(KX,),
        in_specs=[block, whole, whole] + [block] * len(extra),
        out_specs=block,
        out_shape=jax.ShapeDtypeStruct((KX, N, N), jnp.float32),
        name=name,
        cost_estimate=pl.CostEstimate(
            flops=6 * KX * N * N * N, bytes_accessed=2 * KX * N * N * 4, transcendentals=0
        ),
    )(field, *matrices, *extra)


def finish_kernel(starts, places, in_ref, part_ref, sort_ref, out_ref, peak_ref, lined, total, top):
    quad = pl.program_id(0)
    gather_quad(starts, places, in_ref, lined, quad)

    def step(t, carry):
        rows = pl.ds(pl.multiple_of(t * CHUNK, CHUNK), CHUNK)
        turned = turn_lanes([lined[cc, rows, :] for cc in range(4)])
        for k in range(KX):
            total[k, rows, :] = turned[k] + part_ref[k, rows, :]
        return carry

    lax.fori_loop(0, N // CHUNK, step, 0)
    sorter = sort_ref[0]
    for k in range(KX):
        for m in range(2):
            low_rows = total[k, pl.ds(m * 256, LANES), :]
            high_rows = total[k, pl.ds(m * 256 + LANES, LANES), :]
            wide = jnp.concatenate([low_rows, high_rows], axis=1)
            first, second = halves(wide)
            dims = (((1,), (1,)), ((), ()))
            tall = lax.dot_general(
                sorter, first, dims, preferred_element_type=jnp.float32
            ) + lax.dot_general(sorter, second, dims, preferred_element_type=jnp.float32)
            tiles = tall.reshape(32, 8, LANES)
            at = (k * 2 + m) * 8
            out_ref[:, at : at + 8, :] = tiles
            best = jnp.max(jnp.abs(tiles), axis=0)

            @pl.when(quad == 0)
            def _():
                top[at : at + 8, :] = best

            @pl.when(quad != 0)
            def _():
                top[at : at + 8, :] = jnp.maximum(top[at : at + 8, :], best)

    @pl.when(quad == 3)
    def _():
        peak = top[pl.ds(0, 16, stride=4), :]
        for gp in range(1, 4):
            peak = jnp.maximum(peak, top[pl.ds(gp, 16, stride=4), :])
        peak_ref[...] = jnp.broadcast_to(peak[None], peak_ref.shape)


def finish(received, part, sorter, starts, places):
    return pl.pallas_call(
        finish_kernel,
        grid_spec=pltpu.PrefetchScalarGridSpec(
            num_scalar_prefetch=2,
            grid=(4,),
            in_specs=[
                pl.BlockSpec((NR, 4, ROWS, LANES), lambda q, *_: (0, q, 0, 0)),
                pl.BlockSpec((KX, N, LANES), lambda q, *_: (0, 0, q)),
                pl.BlockSpec((1, 256, 256), lambda q, *_: (q, 0, 0)),
            ],
            out_specs=[
                pl.BlockSpec((32, 64, LANES), lambda q, *_: (q, 0, 0)),
                pl.BlockSpec((DEVICES, 16, LANES), lambda q, *_: (0, 0, 0)),
            ],
            scratch_shapes=[
                pltpu.VMEM((4, LINED, LANES), jnp.float32),
                pltpu.VMEM((KX, N, LANES), jnp.float32),
                pltpu.VMEM((64, LANES), jnp.float32),
            ],
        ),
        out_shape=[
            jax.ShapeDtypeStruct((DEVICES, 64, LANES), jnp.float32),
            jax.ShapeDtypeStruct((DEVICES, 16, LANES), jnp.float32),
        ],
        name="finish",
        cost_estimate=pl.CostEstimate(
            flops=4 * N * N * N, bytes_accessed=4 * KX * N * N * 4, transcendentals=0
        ),
    )(starts, places, received.reshape(NR, NB, ROWS, LANES), part, sorter)


def sorters(new_col):
    block = jnp.arange(4, dtype=jnp.int32)
    device = (block // 2)[None, :, None] * 16 + new_col.reshape(4, 4, NB)
    slot = device * 8 + (block % 2)[None, :, None] * 2
    j = jnp.arange(2, dtype=jnp.int32)
    p = jnp.arange(2, dtype=jnp.int32)
    target = slot[:, None, :, :, None] + j[None, :, None, None, None] * 4 + p
    target = target.reshape(4, 1, 256)
    hit = target == jnp.arange(256, dtype=jnp.int32)[None, :, None]
    return hit.astype(jnp.bfloat16)


def unpack_slab_kernel(in_ref, out_ref):
    for j in range(2):
        for gp in range(4):
            out_ref[gp, j * LANES : (j + 1) * LANES, :] = in_ref[:, j * 4 + gp, :].T


def unpack_slab(arrived):
    return pl.pallas_call(
        unpack_slab_kernel,
        grid=(KX, 2),
        in_specs=[pl.BlockSpec((DEVICES, 8, LANES), lambda k, m: (0, k * 2 + m, 0))],
        out_specs=pl.BlockSpec((4, 256, LANES), lambda k, m: (0, m, k)),
        out_shape=jax.ShapeDtypeStruct((4, N, N), jnp.float32),
        name="unpack_slab",
    )(arrived)


def unpack_peak_kernel(in_ref, out_ref):
    for half in range(2):
        for y in range(4):
            out_ref[y * LANES : (y + 1) * LANES, half * LANES : (half + 1) * LANES] = in_ref[
                :, half * 4 + y, :
            ].T


def unpack_peak(arrived):
    return pl.pallas_call(
        unpack_peak_kernel,
        grid=(2,),
        in_specs=[pl.BlockSpec((DEVICES, 8, LANES), lambda t: (0, t, 0))],
        out_specs=pl.BlockSpec((N, 256), lambda t: (0, t)),
        out_shape=jax.ShapeDtypeStruct((N, N), jnp.float32),
        name="unpack_peak",
    )(arrived)


def exchange(value):
    return lax.all_to_all(value, AXES, split_axis=0, concat_axis=0, tiled=True)


def on_device(velocity, y_sizes, old_place, new_col):
    velocity = velocity.reshape(3, ROWS, ZB, N)
    starts = jnp.cumsum(y_sizes) - y_sizes
    matrices = tuple(jnp.asarray(part) for part in spectral_pair())
    sorter = sorters(new_col)
    got_2 = exchange(pack(velocity, 2))
    got_1 = exchange(pack(velocity, 1))
    got_0 = exchange(pack(velocity, 0, matrices))
    part = slopes(slope_z_kernel, gather(got_2, starts, old_place, "gather_2"), matrices, (), "slope_z")
    part = slopes(
        slope_y_kernel, gather(got_1, starts, old_place, "gather_1"), matrices, (part,), "slope_y"
    )
    packed, peaks = finish(got_0, part, sorter, starts, old_place)
    slab = unpack_slab(exchange(packed))
    peak = unpack_peak(exchange(peaks))
    return slab.reshape(2, 1, 2, N, N), peak


def solution(mesh):
    in_specs = (P(None, "col", "row", None, None, None), P(), P(), P())
    out_specs = (P("row", "col", None, None, None), P())
    return jax.shard_map(
        on_device, mesh=mesh, in_specs=in_specs, out_specs=out_specs, check_vma=False
    )
```

time: 794 us -> 327 us (0.41)
  waiting for transfers between devices: 342 us -> 165 us
  local copies, waits for them, and re-layouts: 147 us -> 0.46 us
  blocking collectives: 163 us -> 26.6 us
  Pallas kernels: 0 us -> 97.1 us
  matrix products: 54.7 us -> 0 us
  other arithmetic: 35 us -> 1.97 us
  between operations: 14.6 us -> 0.71 us
    pmax x1 -> x0, waiting for transfers between devices: 144 us -> none  [on_device(): peak = lax.pmax(local_peak, ('row', 'col'))]
    all_to_all x1, blocking collectives: 163 us -> 26.6 us  [exchange(): return lax.all_to_all(value, AXES, split_axis=0, concat_axis=0, tiled=True)]
    pallas_call x0 -> x10, Pallas kernels: none -> 97.1 us  [the longest x3 29.1 us: pack(): pl.pallas_call(pack_plain if matrices is None else pack_slope, grid=(ROWS...]
    gather x8 -> x0, local copies, waits for them, and re-layouts: 72.1 us -> none  [the longest x2 40.1 us: on_device(): picked = jnp.take(flat[:, :, group], my_rows[group], axis=1)]
    dot_general x4 -> x0, matrix products: 54.7 us -> none  [the longest x1 20.6 us: along_rows(): return jnp.einsum('jy,ksyx->ksjx', matrix, field, precision=EXACT)]
    all_to_all x5 -> x4, waiting for transfers between devices: 198 us -> 165 us  [exchange(): return lax.all_to_all(value, AXES, split_axis=0, concat_axis=0, tiled=True)]
    all_to_all x7 -> x0, local copies, waits for them, and re-layouts: 25.1 us -> none  [the longest x4 11.2 us: turn(): lax.all_to_all(slope.reshape(shape), ('row', 'col'), split_axis=0, concat...]
    another operation x2 -> x1, local copies, waits for them, and re-layouts: 16.9 us -> 0.08 us  [the longest x1 16.8 us: on_device(): velocity.reshape(fields, places, row_depth, columns, thick, x_cells)]
  transfers between devices with their start and end apart: 6 -> 4, of which waited for: 6 -> 4; matrix products, arithmetic and copies ran while one was open for 10% -> 1% of each run, Pallas kernels for 0% -> 18%
where the time goes in v1:
time: 327 us; the launch traced here: 325 us
  waiting for transfers between devices  165 us (50%)
  Pallas kernels  97.1 us (30%)
  starting transfers between devices  33.1 us (10%)
  blocking collectives  26.6 us (8%)
    all_to_all x4, waiting for transfers between devices, exchange(): return lax.all_to_all(value, AXES, split_axis=0, concat_axis=0, tiled=True)  165 us
    all_to_all x4, starting transfers between devices, exchange(): return lax.all_to_all(value, AXES, split_axis=0, concat_axis=0, tiled=True)  33.1 us
    pallas_call x3, Pallas kernels, pack(): pl.pallas_call(pack_plain if matrices is None else pack_slope, grid=(ROWS...  29.1 us
    all_to_all x1, blocking collectives, exchange(): return lax.all_to_all(value, AXES, split_axis=0, concat_axis=0, tiled=True)  26.6 us
    pallas_call x2, Pallas kernels, gather(): pl.pallas_call(gather_kernel, grid_spec=pltpu.PrefetchScalarGridSpec(num_...  21.7 us
    pallas_call x1, Pallas kernels, finish(): pl.pallas_call(finish_kernel, grid_spec=pltpu.PrefetchScalarGridSpec(num_...  20.9 us
    pallas_call x2, Pallas kernels, slopes(): pl.pallas_call(kernel, grid=(KX,), in_specs=[block, whole, whole] + [bloc...  15.2 us
    pallas_call x1, Pallas kernels, unpack_slab(): pl.pallas_call(unpack_slab_kernel, grid=(KX, 2), in_specs=[pl.BlockSpec((...  7.64 us
  transfers between devices with their start and end apart: 4, of which 4 were waited for; matrix products, arithmetic and copies ran while one was open for 1% of the time, Pallas kernels for 18%

profile of v1, /device:TPU:0, one launch (start us, length us, event | category | flops | bytes accessed | tf_op | source)
XLA Modules:
  0.0 324.8 jit_solution(14564968704032460888)
XLA Ops:
  0.6 8.8 %pack_2.1 = f32[128,72,128]{2,1,0:T(8,128)} custom-call(f32[3,72,32,512]{3,2,1,0:T(8,128)} %bitcast.12), custom_call_target="tpu_custom_call" | custom-call | flops 1207959552 | bytes 9437184 | tf_op jit(solution)/shard_map/pack_2/pallas_call | solution.py:69
  9.4 11.6 %all-to-all-start.2 = ((f32[128,72,128]{2,1,0:T(8,128)}), f32[128,72,128]{2,1,0:T(8,128)}, u32[]{:S(2)}, u32[]{:S(2)}) async-start(f32[128,72,128]{2,1,0:T(8,128)} %pack_2.1), calls=%async_computation.2 | async-start | bytes 9437184 | tf_op jit(solution)/shard_map/all_to_all | solution.py:294
  21.0 8.7 %pack_1.1 = f32[128,72,128]{2,1,0:T(8,128)} custom-call(f32[3,72,32,512]{3,2,1,0:T(8,128)} %bitcast.13), custom_call_target="tpu_custom_call" | custom-call | flops 1207959552 | bytes 9437184 | tf_op jit(solution)/shard_map/pack_1/pallas_call | solution.py:69
  29.8 49.5 %all-to-all-done.2 = f32[128,72,128]{2,1,0:T(8,128)} async-done(((f32[128,72,128]{2,1,0:T(8,128)}), f32[128,72,128]{2,1,0:T(8,128)}, u32[]{:S(2)}, u32[]{:S(2)}) %all-to-all-start.2) | async-done | bytes 4718624 | tf_op jit(solution)/shard_map/all_to_all | solution.py:294
  79.3 7.8 %all-to-all-start.1 = ((f32[128,72,128]{2,1,0:T(8,128)}), f32[128,72,128]{2,1,0:T(8,128)}, u32[]{:S(2)}, u32[]{:S(2)}) async-start(f32[128,72,128]{2,1,0:T(8,128)} %pack_1.1), calls=%async_computation.1 | async-start | bytes 9437184 | tf_op jit(solution)/shard_map/all_to_all | solution.py:294
  87.1 11.6 %pack_slope.1 = f32[128,72,128]{2,1,0:T(8,128)} custom-call(f32[3,72,32,512]{3,2,1,0:T(8,128)} %bitcast.14, bf16[512,512]{1,0:T(8,128)(2,1)} %constant.43.clone.high_ref, bf16[512,512]{1,0:T(8,128)(2,1)} %constant.44.clone.low_ref), custom_call_target="tpu_custom_call" | custom-call | flops 7247757312 | bytes 9437184 | tf_op jit(solution)/shard_map/pack_slope/pallas_call | solution.py:69
  98.8 46.6 %all-to-all-done.1 = f32[128,72,128]{2,1,0:T(8,128)} async-done(((f32[128,72,128]{2,1,0:T(8,128)}), f32[128,72,128]{2,1,0:T(8,128)}, u32[]{:S(2)}, u32[]{:S(2)}) %all-to-all-start.1) | async-done | bytes 4718624 | tf_op jit(solution)/shard_map/all_to_all | solution.py:294
  145.4 7.8 %all-to-all-start = ((f32[128,72,128]{2,1,0:T(8,128)}), f32[128,72,128]{2,1,0:T(8,128)}, u32[]{:S(2)}, u32[]{:S(2)}) async-start(f32[128,72,128]{2,1,0:T(8,128)} %pack_slope.1), calls=%async_computation | async-start | bytes 9437184 | tf_op jit(solution)/shard_map/all_to_all | solution.py:294
  153.3 0.1 reduce
  153.5 0.6 sub.7.starts
  154.1 0.1 copy.11
  154.2 0.1 add.91
  154.7 1.0 fusion.sort_ref
  155.7 10.9 %gather_2.1.field_ref = f32[4,512,512]{2,1,0:T(8,128)} custom-call(s32[16]{0:T(128)} %sub.7.starts, s32[16,16]{1,0:T(8,128)} %places.5, f32[8,16,72,128]{3,2,1,0:T(8,128)} %bitcast.4.in_ref), custom_call_target="tpu_custom_call" | custom-call | flops 1073741824 | bytes 8388608 | tf_op jit(solution)/shard_map/gather_2/pallas_call | solution.py:128
  166.6 10.8 %gather_1.1.field_ref = f32[4,512,512]{2,1,0:T(8,128)} custom-call(s32[16]{0:T(128)} %sub.7.starts, s32[16,16]{1,0:T(8,128)} %places.5, f32[8,16,72,128]{3,2,1,0:T(8,128)} %bitcast.3.in_ref), custom_call_target="tpu_custom_call" | custom-call | flops 1073741824 | bytes 8388608 | tf_op jit(solution)/shard_map/gather_1/pallas_call | solution.py:128
  177.4 7.2 %slope_z.1.add_ref = f32[4,512,512]{2,1,0:T(8,128)} custom-call(f32[4,512,512]{2,1,0:T(8,128)} %gather_2.1.field_ref, bf16[512,512]{1,0:T(8,128)(2,1)} %constant.43.clone.high_ref, bf16[512,512]{1,0:T(8,128)(2,1)} %constant.44.clone.low_ref), custom_call_target="tpu_custom_call" | custom-call | flops 3221225472 | bytes 8388608 | tf_op jit(solution)/shard_map/slope_z/pallas_call | solution.py:156
  184.6 8.0 %slope_y.1.part_ref = f32[4,512,512]{2,1,0:T(8,128)} custom-call(f32[4,512,512]{2,1,0:T(8,128)} %gather_1.1.field_ref, bf16[512,512]{1,0:T(8,128)(2,1)} %constant.43.clone.high_ref, bf16[512,512]{1,0:T(8,128)(2,1)} %constant.44.clone.low_ref, f32[4,512,512]{2,1,0:T(8,128)} %slope_z.1.add_ref), custom_call_target="tpu_custom_call" | custom-call | flops 3221225472 | bytes 8388608 | tf_op jit(solution)/shard_map/slope_y/pallas_call | solution.py:156
  192.6 18.9 %all-to-all-done = f32[128,72,128]{2,1,0:T(8,128)} async-done(((f32[128,72,128]{2,1,0:T(8,128)}), f32[128,72,128]{2,1,0:T(8,128)}, u32[]{:S(2)}, u32[]{:S(2)}) %all-to-all-start) | async-done | bytes 4718624 | tf_op jit(solution)/shard_map/all_to_all | solution.py:294
  211.5 20.9 %finish.1 = (f32[128,64,128]{2,1,0:T(8,128)}, f32[128,16,128]{2,1,0:T(8,128)}) custom-call(s32[16]{0:T(128)} %sub.7.starts, s32[16,16]{1,0:T(8,128)} %places.5, f32[8,16,72,128]{3,2,1,0:T(8,128)} %bitcast.2.in_ref, f32[4,512,512]{2,1,0:T(8,128)} %slope_y.1.part_ref, bf16[4,256,256]{2,1,0:T(8,128)(2,1)} %fusion.sort_ref), custom_call_target="tpu_custom_call" | custom-call | flops 536870912 | bytes 16777216 | tf_op jit(solution)/shard_map/finish/pallas_call | solution.py:214
  232.3 26.6 %all_to_all.25.in_ref = f32[128,16,128]{2,1,0:T(8,128)} all-to-all(f32[128,16,128]{2,1,0:T(8,128)} %get-tuple-element.5), channel_id=1, replica_groups=mesh['row'=8,'col'=16] {'row','col'}, dimensions={0} | all-to-all | bytes 2097152 | tf_op jit(solution)/shard_map/all_to_all | solution.py:294
  259.0 5.8 %all-to-all-start.3 = ((f32[128,64,128]{2,1,0:T(8,128)}), f32[128,64,128]{2,1,0:T(8,128)}, u32[]{:S(2)}, u32[]{:S(2)}) async-start(f32[128,64,128]{2,1,0:T(8,128)} %get-tuple-element.4), calls=%async_computation.3 | async-start | bytes 8388608 | tf_op jit(solution)/shard_map/all_to_all | solution.py:294
  264.8 2.6 unpack_peak.1
  267.4 49.8 %all-to-all-done.3.in_ref = f32[128,64,128]{2,1,0:T(8,128)} async-done(((f32[128,64,128]{2,1,0:T(8,128)}), f32[128,64,128]{2,1,0:T(8,128)}, u32[]{:S(2)}, u32[]{:S(2)}) %all-to-all-start.3) | async-done | bytes 4194336 | tf_op jit(solution)/shard_map/all_to_all | solution.py:294
  317.2 7.6 %unpack_slab.1 = f32[4,512,512]{2,1,0:T(8,128)} custom-call(f32[128,64,128]{2,1,0:T(8,128)} %all-to-all-done.3.in_ref), custom_call_target="tpu_custom_call" | custom-call | tf_op jit(solution)/shard_map/unpack_slab/pallas_call | solution.py:264
  (14 shorter events, 0.5 us)
Async XLA Ops:
  9.4 69.9 %all-to-all-start.2 = ((f32[128,72,128]{2,1,0:T(8,128)}), f32[128,72,128]{2,1,0:T(8,128)}, u32[]{:S(2)}, u32[]{:S(2)}) async-start(f32[128,72,128]{2,1,0:T(8,128)} %pack_2.1), calls=%async_computation.2 | async-start | bytes 9437184 | tf_op jit(solution)/shard_map/all_to_all | solution.py:294
  79.3 66.1 %all-to-all-start.1 = ((f32[128,72,128]{2,1,0:T(8,128)}), f32[128,72,128]{2,1,0:T(8,128)}, u32[]{:S(2)}, u32[]{:S(2)}) async-start(f32[128,72,128]{2,1,0:T(8,128)} %pack_1.1), calls=%async_computation.1 | async-start | bytes 9437184 | tf_op jit(solution)/shard_map/all_to_all | solution.py:294
  98.8 54.4 %copy-start.1 = (s32[16]{0:T(128)S(1)}, s32[16]{0:T(128)}, u32[]{:S(2)}) copy-start(s32[16]{0:T(128)} %param.7) | copy-start | bytes 196
  98.8 55.3 %copy-start = (s32[16,16]{1,0:T(8,128)S(1)}, s32[16,16]{1,0:T(8,128)}, u32[]{:S(2)}) copy-start(s32[16,16]{1,0:T(8,128)} %param.9) | copy-start | bytes 3076
  145.4 66.1 %all-to-all-start = ((f32[128,72,128]{2,1,0:T(8,128)}), f32[128,72,128]{2,1,0:T(8,128)}, u32[]{:S(2)}, u32[]{:S(2)}) async-start(f32[128,72,128]{2,1,0:T(8,128)} %pack_slope.1), calls=%async_computation | async-start | bytes 9437184 | tf_op jit(solution)/shard_map/all_to_all | solution.py:294
  259.0 58.2 %all-to-all-start.3 = ((f32[128,64,128]{2,1,0:T(8,128)}), f32[128,64,128]{2,1,0:T(8,128)}, u32[]{:S(2)}, u32[]{:S(2)}) async-start(f32[128,64,128]{2,1,0:T(8,128)} %get-tuple-element.4), calls=%async_computation.3 | async-start | bytes 8388608 | tf_op jit(solution)/shard_map/all_to_all | solution.py:294

commit v2 on v1

v2 whole, which is shorter than its diff:
```python
import jax
import jax.numpy as jnp
import numpy as np
from jax import lax
from jax.experimental import pallas as pl
from jax.experimental.pallas import tpu as pltpu
from jax.sharding import PartitionSpec as P

AXES = ("col", "row")
LANES = 128
N = 512
DEVICES = 128
KX = N // DEVICES
ROWS = 72
CAP = 36
PLACED = 80
ZB = 32
NB = 16
NR = 8


def spectral_pair():
    gap = (np.arange(N)[:, None] - np.arange(N)[None, :]) % N
    angle = gap * (np.pi / N)
    parity = 1.0 - 2.0 * (gap % 2)
    safe = np.where(gap == 0, 1.0, np.sin(angle))
    full = np.where(gap == 0, 0.0, parity * np.cos(angle) / safe * (2.0 / N))
    full = (full - full.T) / 2
    high = full.astype(jnp.bfloat16)
    low = (full - high.astype(np.float64)).astype(jnp.bfloat16)
    return high, low


def halves(value):
    high = value.astype(jnp.bfloat16)
    return high, (value - high.astype(jnp.float32)).astype(jnp.bfloat16)


def mul(left, right):
    return jnp.dot(left, right, preferred_element_type=jnp.float32)


def mul3(left, right):
    return mul(left[0], right[0]) + (mul(left[1], right[0]) + mul(left[0], right[1]))


def pack_rows(value, out_ref, i):
    tall = jnp.concatenate([value[:, k * LANES : (k + 1) * LANES] for k in range(KX)], axis=0)
    out_ref[:, i, :] = tall.T


FIELDS = (2, 1)
STEPS = ROWS // 8


def pack_pair_kernel(in_ref, out_ref, taken, made, in_sem, out_sem):
    def load(step):
        field, t = divmod(step, STEPS)
        return pltpu.make_async_copy(
            in_ref.at[FIELDS[field], pl.ds(t * 8, 8)], taken.at[step], in_sem.at[step]
        )

    def store(step):
        return pltpu.make_async_copy(
            made.at[step], out_ref.at[:, pl.ds(step * 8, 8), :], out_sem.at[step]
        )

    total = STEPS * len(FIELDS)
    for step in range(total):
        load(step).start()
    for step in range(total):
        load(step).wait()
        for i in range(8):
            pack_rows(taken[step, i], made.at[step], i)
        store(step).start()
    for step in range(total):
        store(step).wait()


def pack_pair(velocity):
    total = STEPS * len(FIELDS)
    return pl.pallas_call(
        pack_pair_kernel,
        in_specs=[pl.BlockSpec(memory_space=pl.ANY)],
        out_specs=pl.BlockSpec(memory_space=pl.ANY),
        out_shape=jax.ShapeDtypeStruct((DEVICES, total * 8, LANES), jnp.float32),
        scratch_shapes=[
            pltpu.VMEM((total, 8, ZB, N), jnp.float32),
            pltpu.VMEM((total, DEVICES, 8, LANES), jnp.float32),
            pltpu.SemaphoreType.DMA((total,)),
            pltpu.SemaphoreType.DMA((total,)),
        ],
        name="pack_pair",
        cost_estimate=pl.CostEstimate(
            flops=2 * ROWS * ZB * N * N, bytes_accessed=4 * ROWS * ZB * N * 4, transcendentals=0
        ),
    )(velocity)


def pack_slope(in_ref, high_ref, low_ref, out_ref):
    flat = in_ref[0].reshape(8 * ZB, N)
    slope = -mul3(halves(flat), (high_ref[...], low_ref[...]))
    for i in range(8):
        pack_rows(slope[i * ZB : (i + 1) * ZB], out_ref, i)


def pack_derived(velocity, matrices):
    return pl.pallas_call(
        pack_slope,
        grid=(STEPS,),
        in_specs=[pl.BlockSpec((1, 8, ZB, N), lambda t: (0, t, 0, 0))]
        + [pl.BlockSpec((N, N), lambda t: (0, 0))] * 2,
        out_specs=pl.BlockSpec((DEVICES, 8, LANES), lambda t: (0, t, 0)),
        out_shape=jax.ShapeDtypeStruct((DEVICES, ROWS, LANES), jnp.float32),
        name="pack_slope",
        cost_estimate=pl.CostEstimate(
            flops=6 * ROWS * ZB * N * N, bytes_accessed=2 * ROWS * ZB * N * 4, transcendentals=0
        ),
    )(velocity, *matrices)


def gather_quad(starts, places, in_ref, lined, quad, first=0):
    for cc in range(4):
        for b in range(NB):
            place = places[quad * 4 + cc, b]
            source = in_ref[first + cc, place // 2, pl.ds((place % 2) * CAP, CAP), :]
            lined[cc, pl.ds(starts[b], CAP), :] = source


def turn_lanes(parts):
    lane = lax.broadcasted_iota(jnp.int32, parts[0].shape, 1)
    upper = (lane // 64) == 1
    odd = (lane // 32) % 2 == 1
    a0, a1, a2, a3 = parts
    b0 = jnp.where(upper, pltpu.roll(a2, 64, 1), a0)
    b2 = jnp.where(upper, a2, pltpu.roll(a0, 64, 1))
    b1 = jnp.where(upper, pltpu.roll(a3, 64, 1), a1)
    b3 = jnp.where(upper, a3, pltpu.roll(a1, 64, 1))
    c0 = jnp.where(odd, pltpu.roll(b1, 32, 1), b0)
    c1 = jnp.where(odd, b1, pltpu.roll(b0, 96, 1))
    c2 = jnp.where(odd, pltpu.roll(b3, 32, 1), b2)
    c3 = jnp.where(odd, b3, pltpu.roll(b2, 96, 1))
    return c0, c1, c2, c3


CHUNK = 64


def gather_kernel(starts, places, in_ref, out_ref, lined):
    gather_quad(starts, places, in_ref, lined, pl.program_id(0))

    def step(t, carry):
        rows = pl.ds(pl.multiple_of(t * CHUNK, CHUNK), CHUNK)
        turned = turn_lanes([lined[cc, rows, :] for cc in range(4)])
        for k in range(KX):
            out_ref[k, rows, :] = turned[k]
        return carry

    lax.fori_loop(0, N // CHUNK, step, 0)


LINED = 560


def gather(received, field, starts, places, name):
    return pl.pallas_call(
        gather_kernel,
        grid_spec=pltpu.PrefetchScalarGridSpec(
            num_scalar_prefetch=2,
            grid=(4,),
            in_specs=[pl.BlockSpec((4, NR, ROWS, LANES), lambda q, *_: (q, 0, field, 0))],
            out_specs=pl.BlockSpec((KX, N, LANES), lambda q, *_: (0, 0, q)),
            scratch_shapes=[pltpu.VMEM((4, LINED, LANES), jnp.float32)],
        ),
        out_shape=jax.ShapeDtypeStruct((KX, N, N), jnp.float32),
        name=name,
        cost_estimate=pl.CostEstimate(
            flops=2 * N * N * N * 4, bytes_accessed=2 * KX * N * N * 4, transcendentals=0
        ),
    )(starts, places, received.reshape(NB, NR, -1, LANES))


def slope_z_kernel(field_ref, high_ref, low_ref, out_ref):
    out_ref[0] = -mul3(halves(field_ref[0]), (high_ref[...], low_ref[...]))


def slope_y_kernel(field_ref, high_ref, low_ref, add_ref, out_ref):
    total = add_ref[0] + mul3((high_ref[...], low_ref[...]), halves(field_ref[0]))
    for quad in range(4):
        out_ref[quad, 0] = total[:, quad * LANES : (quad + 1) * LANES]


BLOCK = pl.BlockSpec((1, N, N), lambda k: (k, 0, 0))
WHOLE = pl.BlockSpec((N, N), lambda k: (0, 0))
COST = pl.CostEstimate(
    flops=6 * KX * N * N * N, bytes_accessed=2 * KX * N * N * 4, transcendentals=0
)


def slope_z(field, matrices):
    return pl.pallas_call(
        slope_z_kernel,
        grid=(KX,),
        in_specs=[BLOCK, WHOLE, WHOLE],
        out_specs=BLOCK,
        out_shape=jax.ShapeDtypeStruct((KX, N, N), jnp.float32),
        name="slope_z",
        cost_estimate=COST,
    )(field, *matrices)


def slope_y(field, matrices, other):
    return pl.pallas_call(
        slope_y_kernel,
        grid=(KX,),
        in_specs=[BLOCK, WHOLE, WHOLE, BLOCK],
        out_specs=pl.BlockSpec((4, 1, N, LANES), lambda k: (0, k, 0, 0)),
        out_shape=jax.ShapeDtypeStruct((4, KX, N, LANES), jnp.float32),
        name="slope_y",
        cost_estimate=COST,
    )(field, *matrices, other)


def finish_kernel(
    starts, places, order_ref, in_ref, part_ref, out_ref,
    taken, part, lined, total, made, top, spread, in_sem, part_sem, out_sem, peak_sem,
):
    def load(quad):
        return (
            pltpu.make_async_copy(
                in_ref.at[pl.ds(quad * 4, 4)], taken.at[pl.ds(quad * 4, 4)], in_sem.at[quad]
            ),
            pltpu.make_async_copy(part_ref.at[quad], part.at[quad], part_sem.at[quad]),
        )

    def store(quad, side):
        return pltpu.make_async_copy(
            made.at[quad, pl.ds(side * NB, NB), pl.ds(0, 64), :],
            out_ref.at[:, quad * 2 + side, pl.ds(0, 64), :],
            out_sem.at[quad, side],
        )

    for quad in range(4):
        for copy in load(quad):
            copy.start()
    top[...] = jnp.zeros_like(top)

    def one(quad, carry):
        for copy in load(quad):
            copy.wait()
        gather_quad(starts, places, taken, lined, quad, quad * 4)
        order = jnp.broadcast_to(order_ref[pl.ds(quad, 1), :], (CHUNK, LANES))

        def step(t, carry):
            rows = pl.ds(pl.multiple_of(t * CHUNK, CHUNK), CHUNK)
            turned = turn_lanes([lined[cc, rows, :] for cc in range(4)])
            for k in range(KX):
                value = turned[k] + part[quad, k, rows, :]
                total[k, rows, :] = jnp.take_along_axis(value, order, axis=1)
            return carry

        lax.fori_loop(0, N // CHUNK, step, 0)
        for k in range(KX):
            for yb in range(4):
                tile = total[k, yb * LANES : (yb + 1) * LANES, :].T
                at = k * 4 + yb
                for gp in range(4):
                    made[quad, :, at * 4 + gp, :] = tile[gp * 32 : (gp + 1) * 32, :]
                best = jnp.max(jnp.abs(tile).reshape(16, 8, LANES), axis=0)
                top[at * 8 : at * 8 + 8, :] = jnp.maximum(top[at * 8 : at * 8 + 8, :], best)
        for side in range(2):
            store(quad, side).start()
        return carry

    lax.fori_loop(0, 4, one, 0)
    peak = jnp.max(top[...].reshape(16, 8, LANES), axis=1)
    spread[...] = jnp.broadcast_to(peak[None, None], spread.shape)
    last = pltpu.make_async_copy(spread, out_ref.at[:, :, pl.ds(64, 16), :], peak_sem)
    last.start()
    for quad in range(4):
        for side in range(2):
            store(quad, side).wait()
    last.wait()


MADE = 72


def finish(received, part, order, starts, places):
    anywhere = pl.BlockSpec(memory_space=pl.ANY)
    return pl.pallas_call(
        finish_kernel,
        grid_spec=pltpu.PrefetchScalarGridSpec(
            num_scalar_prefetch=2,
            grid=(1,),
            in_specs=[pl.BlockSpec((4, LANES), lambda i, *_: (0, 0)), anywhere, anywhere],
            out_specs=anywhere,
            scratch_shapes=[
                pltpu.VMEM((NB, NR, ROWS, LANES), jnp.float32),
                pltpu.VMEM((4, KX, N, LANES), jnp.float32),
                pltpu.VMEM((4, LINED, LANES), jnp.float32),
                pltpu.VMEM((KX, N, LANES), jnp.float32),
                pltpu.VMEM((4, 32, MADE, LANES), jnp.float32),
                pltpu.VMEM((LANES, LANES), jnp.float32),
                pltpu.VMEM((NB, NR, 16, LANES), jnp.float32),
                pltpu.SemaphoreType.DMA((4,)),
                pltpu.SemaphoreType.DMA((4,)),
                pltpu.SemaphoreType.DMA((4, 2)),
                pltpu.SemaphoreType.DMA,
            ],
        ),
        out_shape=jax.ShapeDtypeStruct((NB, NR, PLACED, LANES), jnp.float32),
        name="finish",
        cost_estimate=pl.CostEstimate(
            flops=4 * N * N * N, bytes_accessed=4 * KX * N * N * 4, transcendentals=0
        ),
    )(starts, places, order, received.reshape(NB, NR, ROWS, LANES), part)


def lane_order(new_col):
    slab = jnp.arange(NB, dtype=jnp.int32)
    hits = (new_col[:, :, None] == slab[None, None, :]).astype(jnp.int32)
    slab_of = jnp.sum(hits * slab[None, :, None], axis=1).reshape(4, 2, 2, NB)
    block = jnp.arange(4, dtype=jnp.int32).reshape(1, 2, 2, 1)
    lane = block * ZB + slab_of * 2
    lane = jnp.swapaxes(lane, 1, 2)[:, :, None] + jnp.arange(2, dtype=jnp.int32)[:, None, None]
    return lane.reshape(4, LANES)


def unpack_kernel(in_ref, slab_ref, peak_ref, taken, slab, peak, in_sem, slab_sem, peak_sem):
    def load(t):
        return pltpu.make_async_copy(
            in_ref.at[:, pl.ds(t * 8, 8), :], taken.at[t], in_sem.at[t]
        )

    def store(t):
        k, m = divmod(t, 2)
        return pltpu.make_async_copy(
            slab.at[t],
            slab_ref.at[:, pl.ds(m * 256, 256), pl.ds(k * LANES, LANES)],
            slab_sem.at[t],
        )

    def store_peak(t):
        return pltpu.make_async_copy(
            peak.at[t], peak_ref.at[:, pl.ds(t * 256, 256)], peak_sem.at[t]
        )

    for t in range(10):
        load(t).start()
    for t in range(8):
        load(t).wait()
        for j in range(2):
            for gp in range(4):
                slab[t, gp, j * LANES : (j + 1) * LANES, :] = taken[t, :, j * 4 + gp, :].T
        store(t).start()
    for t in range(2):
        load(8 + t).wait()
        for half in range(2):
            for yb in range(4):
                peak[t, yb * LANES : (yb + 1) * LANES, half * LANES : (half + 1) * LANES] = (
                    taken[8 + t, :, half * 4 + yb, :].T
                )
        store_peak(t).start()
    for t in range(8):
        store(t).wait()
    for t in range(2):
        store_peak(t).wait()


def unpack(arrived):
    anywhere = pl.BlockSpec(memory_space=pl.ANY)
    return pl.pallas_call(
        unpack_kernel,
        in_specs=[anywhere],
        out_specs=[anywhere, anywhere],
        out_shape=[
            jax.ShapeDtypeStruct((4, N, N), jnp.float32),
            jax.ShapeDtypeStruct((N, N), jnp.float32),
        ],
        scratch_shapes=[
            pltpu.VMEM((10, DEVICES, 8, LANES), jnp.float32),
            pltpu.VMEM((8, 4, 256, LANES), jnp.float32),
            pltpu.VMEM((2, N, 256), jnp.float32),
            pltpu.SemaphoreType.DMA((10,)),
            pltpu.SemaphoreType.DMA((8,)),
            pltpu.SemaphoreType.DMA((2,)),
        ],
        name="unpack",
    )(arrived)


def exchange(value):
    return lax.all_to_all(value, AXES, split_axis=0, concat_axis=0, tiled=True)


def on_device(velocity, y_sizes, old_place, new_col):
    velocity = velocity.reshape(3, ROWS, ZB, N)
    starts = jnp.cumsum(y_sizes) - y_sizes
    matrices = tuple(jnp.asarray(part) for part in spectral_pair())
    order = lane_order(new_col)
    pair = exchange(pack_pair(velocity))
    derived = exchange(pack_derived(velocity, matrices))
    part = slope_z(gather(pair, 0, starts, old_place, "gather_2"), matrices)
    part = slope_y(gather(pair, 1, starts, old_place, "gather_1"), matrices, part)
    packed = finish(derived, part, order, starts, old_place)
    slab, peak = unpack(exchange(packed.reshape(DEVICES, PLACED, LANES)))
    return slab.reshape(2, 1, 2, N, N), peak


def solution(mesh):
    in_specs = (P(None, "col", "row", None, None, None), P(), P(), P())
    out_specs = (P("row", "col", None, None, None), P())
    return jax.shard_map(
        on_device, mesh=mesh, in_specs=in_specs, out_specs=out_specs, check_vma=False
    )
```

time: 327 us -> 295 us (0.902)
  blocking collectives: 26.6 us -> 69.9 us
  waiting for transfers between devices: 165 us -> 124 us
  Pallas kernels: 97.1 us -> 79.7 us
  starting transfers between devices: 33.1 us -> 17.8 us
    all_to_all x1, blocking collectives: 26.6 us -> 69.9 us  [exchange(): return lax.all_to_all(value, AXES, split_axis=0, concat_axis=0, tiled=True)]
    all_to_all x4 -> x2, waiting for transfers between devices: 165 us -> 124 us  [exchange(): return lax.all_to_all(value, AXES, split_axis=0, concat_axis=0, tiled=True)]
    all_to_all x4 -> x2, starting transfers between devices: 33.1 us -> 17.8 us  [exchange(): return lax.all_to_all(value, AXES, split_axis=0, concat_axis=0, tiled=True)]
    pallas_call x7 -> x5, Pallas kernels: 54.5 us -> 40.9 us  [the longest x1 11.6 us: pack_derived(): pl.pallas_call(pack_slope, grid=(STEPS,), in_specs=[pl.BlockSpec((1, 8, Z...]
    pallas_call x1, Pallas kernels: 20.9 us -> 17.1 us  [finish(): pl.pallas_call(finish_kernel, grid_spec=pltpu.PrefetchScalarGridSpec(num_...]
  transfers between devices with their start and end apart: 4 -> 2, of which waited for: 4 -> 2; matrix products, arithmetic and copies ran while one was open for 1% -> 1% of each run, Pallas kernels for 18% -> 16%
where the time goes in v2:
time: 295 us; the launch traced here: 294 us
  waiting for transfers between devices  124 us (42%)
  Pallas kernels  79.7 us (27%)
  blocking collectives  69.9 us (24%)
  starting transfers between devices  17.8 us (6%)
    all_to_all x2, waiting for transfers between devices, exchange(): return lax.all_to_all(value, AXES, split_axis=0, concat_axis=0, tiled=True)  124 us
    all_to_all x1, blocking collectives, exchange(): return lax.all_to_all(value, AXES, split_axis=0, concat_axis=0, tiled=True)  69.9 us
    pallas_call x2, Pallas kernels, gather(): pl.pallas_call(gather_kernel, grid_spec=pltpu.PrefetchScalarGridSpec(num_...  21.8 us
    all_to_all x2, starting transfers between devices, exchange(): return lax.all_to_all(value, AXES, split_axis=0, concat_axis=0, tiled=True)  17.8 us
    pallas_call x1, Pallas kernels, finish(): pl.pallas_call(finish_kernel, grid_spec=pltpu.PrefetchScalarGridSpec(num_...  17.1 us
    pallas_call x1, Pallas kernels, pack_derived(): pl.pallas_call(pack_slope, grid=(STEPS,), in_specs=[pl.BlockSpec((1, 8, Z...  11.6 us
    pallas_call x1, Pallas kernels, pack_pair(): pl.pallas_call(pack_pair_kernel, in_specs=[pl.BlockSpec(memory_space=pl.A...  8.65 us
    pallas_call x1, Pallas kernels, slope_y(): pl.pallas_call(slope_y_kernel, grid=(KX,), in_specs=[BLOCK, WHOLE, WHOLE,...  7.97 us
  transfers between devices with their start and end apart: 2, of which 2 were waited for; matrix products, arithmetic and copies ran while one was open for 1% of the time, Pallas kernels for 16%

profile of v2, /device:TPU:0, one launch (start us, length us, event | category | flops | bytes accessed | tf_op | source)
XLA Modules:
  0.0 294.1 jit_solution(10996723606719416998)
XLA Ops:
  0.6 8.7 %pack_pair.1 = f32[128,144,128]{2,1,0:T(8,128)} custom-call(f32[3,72,32,512]{3,2,1,0:T(8,128)} %bitcast.11), custom_call_target="tpu_custom_call" | custom-call | flops 1207959552 | bytes 18874368 | tf_op jit(solution)/shard_map/pack_pair/pallas_call | solution.py:82
  9.3 11.6 %all-to-all-start.1 = ((f32[128,144,128]{2,1,0:T(8,128)}), f32[128,144,128]{2,1,0:T(8,128)}, u32[]{:S(2)}, u32[]{:S(2)}) async-start(f32[128,144,128]{2,1,0:T(8,128)} %pack_pair.1), calls=%async_computation.1 | async-start | bytes 18874368 | tf_op jit(solution)/shard_map/all_to_all | solution.py:394
  20.9 11.6 %pack_slope.1 = f32[128,72,128]{2,1,0:T(8,128)} custom-call(f32[3,72,32,512]{3,2,1,0:T(8,128)} %bitcast.12, bf16[512,512]{1,0:T(8,128)(2,1)} %constant.15.clone.high_ref, bf16[512,512]{1,0:T(8,128)(2,1)} %constant.16.clone.low_ref), custom_call_target="tpu_custom_call" | custom-call | flops 3623878656 | bytes 9437184 | tf_op jit(solution)/shard_map/pack_slope/pallas_call | solution.py:108
  32.6 0.0 copy-start.1
  32.6 105.2 %all-to-all-done.1 = f32[128,144,128]{2,1,0:T(8,128)} async-done(((f32[128,144,128]{2,1,0:T(8,128)}), f32[128,144,128]{2,1,0:T(8,128)}, u32[]{:S(2)}, u32[]{:S(2)}) %all-to-all-start.1) | async-done | bytes 9437216 | tf_op jit(solution)/shard_map/all_to_all | solution.py:394
  137.8 6.2 %all-to-all-start = ((f32[128,72,128]{2,1,0:T(8,128)}), f32[128,72,128]{2,1,0:T(8,128)}, u32[]{:S(2)}, u32[]{:S(2)}) async-start(f32[128,72,128]{2,1,0:T(8,128)} %pack_slope.1), calls=%async_computation | async-start | bytes 9437184 | tf_op jit(solution)/shard_map/all_to_all | solution.py:394
  144.0 0.0 copy-done.1
  144.0 0.1 copy.13
  144.1 0.1 reduce
  144.2 0.6 sub.3.starts
  144.8 0.0 copy-done
  144.8 0.1 select_reduce_fusion
  145.0 0.1 add_bitcast_fusion
  145.1 0.1 add.37
  145.1 0.1 add.39
  145.2 0.6 broadcast_add_fusion.order_ref
  145.8 10.9 %gather_2.1.field_ref = f32[4,512,512]{2,1,0:T(8,128)} custom-call(s32[16]{0:T(128)} %sub.3.starts, s32[16,16]{1,0:T(8,128)} %places.5, f32[16,8,144,128]{3,2,1,0:T(8,128)} %bitcast.5.in_ref), custom_call_target="tpu_custom_call" | custom-call | flops 1073741824 | bytes 8388608 | tf_op jit(solution)/shard_map/gather_2/pallas_call | solution.py:166
  156.7 10.9 %gather_1.1.field_ref = f32[4,512,512]{2,1,0:T(8,128)} custom-call(s32[16]{0:T(128)} %sub.3.starts, s32[16,16]{1,0:T(8,128)} %places.5, f32[16,8,144,128]{3,2,1,0:T(8,128)} %bitcast.5.in_ref), custom_call_target="tpu_custom_call" | custom-call | flops 1073741824 | bytes 8388608 | tf_op jit(solution)/shard_map/gather_1/pallas_call | solution.py:166
  167.6 7.2 %slope_z.1.add_ref = f32[4,512,512]{2,1,0:T(8,128)} custom-call(f32[4,512,512]{2,1,0:T(8,128)} %gather_2.1.field_ref, bf16[512,512]{1,0:T(8,128)(2,1)} %constant.15.clone.high_ref, bf16[512,512]{1,0:T(8,128)(2,1)} %constant.16.clone.low_ref), custom_call_target="tpu_custom_call" | custom-call | flops 3221225472 | bytes 8388608 | tf_op jit(solution)/shard_map/slope_z/pallas_call | solution.py:201
  174.7 8.0 %slope_y.1.part_ref = f32[4,4,512,128]{3,2,1,0:T(8,128)} custom-call(f32[4,512,512]{2,1,0:T(8,128)} %gather_1.1.field_ref, bf16[512,512]{1,0:T(8,128)(2,1)} %constant.15.clone.high_ref, bf16[512,512]{1,0:T(8,128)(2,1)} %constant.16.clone.low_ref, f32[4,512,512]{2,1,0:T(8,128)} %slope_z.1.add_ref), custom_call_target="tpu_custom_call" | custom-call | flops 3221225472 | bytes 8388608 | tf_op jit(solution)/shard_map/slope_y/pallas_call | solution.py:213
  182.7 18.8 %all-to-all-done = f32[128,72,128]{2,1,0:T(8,128)} async-done(((f32[128,72,128]{2,1,0:T(8,128)}), f32[128,72,128]{2,1,0:T(8,128)}, u32[]{:S(2)}, u32[]{:S(2)}) %all-to-all-start) | async-done | bytes 4718624 | tf_op jit(solution)/shard_map/all_to_all | solution.py:394
  201.5 17.1 %finish.1 = f32[16,8,80,128]{3,2,1,0:T(8,128)} custom-call(s32[16]{0:T(128)} %sub.3.starts, s32[16,16]{1,0:T(8,128)} %places.5, s32[4,128]{1,0:T(4,128)} %broadcast_add_fusion.order_ref, f32[16,8,72,128]{3,2,1,0:T(8,128)} %bitcast.4.in_ref, f32[4,4,512,128]{3,2,1,0:T(8,128)} %slope_y.1.part_ref), custom_call_target="tpu_custom_call" | custom-call | flops 536870912 | bytes 16777216 | tf_op jit(solution)/shard_map/finish/pallas_call | solution.py:291
  218.6 69.9 %all_to_all.15.in_ref = f32[128,80,128]{2,1,0:T(8,128)} all-to-all(f32[128,80,128]{2,1,0:T(8,128)} %bitcast.13), channel_id=1, replica_groups=mesh['row'=8,'col'=16] {'col','row'}, dimensions={0} | all-to-all | bytes 10485760 | tf_op jit(solution)/shard_map/all_to_all | solution.py:394
  288.5 5.5 %unpack.1 = (f32[4,512,512]{2,1,0:T(8,128)}, f32[512,512]{1,0:T(8,128)}) custom-call(f32[128,80,128]{2,1,0:T(8,128)} %all_to_all.15.in_ref), custom_call_target="tpu_custom_call" | custom-call | tf_op jit(solution)/shard_map/unpack/pallas_call | solution.py:373
  (7 shorter events, 0.1 us)
Async XLA Ops:
  9.3 128.5 %all-to-all-start.1 = ((f32[128,144,128]{2,1,0:T(8,128)}), f32[128,144,128]{2,1,0:T(8,128)}, u32[]{:S(2)}, u32[]{:S(2)}) async-start(f32[128,144,128]{2,1,0:T(8,128)} %pack_pair.1), calls=%async_computation.1 | async-start | bytes 18874368 | tf_op jit(solution)/shard_map/all_to_all | solution.py:394
  32.6 111.4 %copy-start.1 = (s32[16]{0:T(128)S(1)}, s32[16]{0:T(128)}, u32[]{:S(2)}) copy-start(s32[16]{0:T(128)} %param.7) | copy-start | bytes 196
  32.6 112.3 %copy-start = (s32[16,16]{1,0:T(8,128)S(1)}, s32[16,16]{1,0:T(8,128)}, u32[]{:S(2)}) copy-start(s32[16,16]{1,0:T(8,128)} %param.9) | copy-start | bytes 3076
  137.8 63.7 %all-to-all-start = ((f32[128,72,128]{2,1,0:T(8,128)}), f32[128,72,128]{2,1,0:T(8,128)}, u32[]{:S(2)}, u32[]{:S(2)}) async-start(f32[128,72,128]{2,1,0:T(8,128)} %pack_slope.1), calls=%async_computation | async-start | bytes 9437184 | tf_op jit(solution)/shard_map/all_to_all | solution.py:394

commit v3 on v2

--- a/solution.py
+++ b/solution.py
@@ -46,7 +46,7 @@
 
 def pack_rows(value, out_ref, i):
     tall = jnp.concatenate([value[:, k * LANES : (k + 1) * LANES] for k in range(KX)], axis=0)
-    out_ref[:, i, :] = tall.T
+    out_ref[pl.ds(i, DEVICES, stride=8), :] = tall.T
 
 
 FIELDS = (2, 1)
@@ -71,7 +71,7 @@
     for step in range(total):
         load(step).wait()
         for i in range(8):
-            pack_rows(taken[step, i], made.at[step], i)
+            pack_rows(taken[step, i], made.at[step].reshape(DEVICES * 8, LANES), i)
         store(step).start()
     for step in range(total):
         store(step).wait()
@@ -81,8 +81,8 @@
     total = STEPS * len(FIELDS)
     return pl.pallas_call(
         pack_pair_kernel,
-        in_specs=[pl.BlockSpec(memory_space=pl.ANY)],
-        out_specs=pl.BlockSpec(memory_space=pl.ANY),
+        in_specs=[pl.BlockSpec(memory_space=pltpu.HBM)],
+        out_specs=pl.BlockSpec(memory_space=pltpu.HBM),
         out_shape=jax.ShapeDtypeStruct((DEVICES, total * 8, LANES), jnp.float32),
         scratch_shapes=[
             pltpu.VMEM((total, 8, ZB, N), jnp.float32),
@@ -101,7 +101,7 @@
     flat = in_ref[0].reshape(8 * ZB, N)
     slope = -mul3(halves(flat), (high_ref[...], low_ref[...]))
     for i in range(8):
-        pack_rows(slope[i * ZB : (i + 1) * ZB], out_ref, i)
+        pack_rows(slope[i * ZB : (i + 1) * ZB], out_ref.reshape(DEVICES * 8, LANES), i)
 
 
 def pack_derived(velocity, matrices):
@@ -122,8 +122,7 @@
 def gather_quad(starts, places, in_ref, lined, quad, first=0):
     for cc in range(4):
         for b in range(NB):
-            place = places[quad * 4 + cc, b]
-            source = in_ref[first + cc, place // 2, pl.ds((place % 2) * CAP, CAP), :]
+            source = in_ref[first + cc, pl.ds(places[quad * 4 + cc, b], CAP), :]
             lined[cc, pl.ds(starts[b], CAP), :] = source
 
 
@@ -143,11 +142,12 @@
     return c0, c1, c2, c3
 
 
-CHUNK = 64
+CHUNK = 512
 
 
 def gather_kernel(starts, places, in_ref, out_ref, lined):
-    gather_quad(starts, places, in_ref, lined, pl.program_id(0))
+    flat = in_ref.reshape(4, NR * ROWS, LANES)
+    gather_quad(starts, places, flat, lined, pl.program_id(0))
 
     def step(t, carry):
         rows = pl.ds(pl.multiple_of(t * CHUNK, CHUNK), CHUNK)
@@ -248,7 +248,7 @@
     def one(quad, carry):
         for copy in load(quad):
             copy.wait()
-        gather_quad(starts, places, taken, lined, quad, quad * 4)
+        gather_quad(starts, places, taken.reshape(NB, NR * ROWS, LANES), lined, quad, quad * 4)
         order = jnp.broadcast_to(order_ref[pl.ds(quad, 1), :], (CHUNK, LANES))
 
         def step(t, carry):
@@ -264,8 +264,9 @@
             for yb in range(4):
                 tile = total[k, yb * LANES : (yb + 1) * LANES, :].T
                 at = k * 4 + yb
+                flat = made.at[quad].reshape(32 * MADE, LANES)
                 for gp in range(4):
-                    made[quad, :, at * 4 + gp, :] = tile[gp * 32 : (gp + 1) * 32, :]
+                    flat[pl.ds(at * 4 + gp, 32, stride=MADE), :] = tile[gp * 32 : (gp + 1) * 32, :]
                 best = jnp.max(jnp.abs(tile).reshape(16, 8, LANES), axis=0)
                 top[at * 8 : at * 8 + 8, :] = jnp.maximum(top[at * 8 : at * 8 + 8, :], best)
         for side in range(2):
@@ -288,12 +289,13 @@
 
 def finish(received, part, order, starts, places):
     anywhere = pl.BlockSpec(memory_space=pl.ANY)
+    far = pl.BlockSpec(memory_space=pltpu.HBM)
     return pl.pallas_call(
         finish_kernel,
         grid_spec=pltpu.PrefetchScalarGridSpec(
             num_scalar_prefetch=2,
             grid=(1,),
-            in_specs=[pl.BlockSpec((4, LANES), lambda i, *_: (0, 0)), anywhere, anywhere],
+            in_specs=[pl.BlockSpec((4, LANES), lambda i, *_: (0, 0)), far, far],
             out_specs=anywhere,
             scratch_shapes=[
                 pltpu.VMEM((NB, NR, ROWS, LANES), jnp.float32),
@@ -311,6 +313,7 @@
         ),
         out_shape=jax.ShapeDtypeStruct((NB, NR, PLACED, LANES), jnp.float32),
         name="finish",
+        compiler_params=pltpu.CompilerParams(vmem_limit_bytes=57 << 20),
         cost_estimate=pl.CostEstimate(
             flops=4 * N * N * N, bytes_accessed=4 * KX * N * N * 4, transcendentals=0
         ),
@@ -346,20 +349,24 @@
             peak.at[t], peak_ref.at[:, pl.ds(t * 256, 256)], peak_sem.at[t]
         )
 
+    def turn(t, row):
+        flat = taken.at[t].reshape(DEVICES * 8, LANES)
+        return flat[pl.ds(row, DEVICES, stride=8), :].T
+
     for t in range(10):
         load(t).start()
     for t in range(8):
         load(t).wait()
         for j in range(2):
             for gp in range(4):
-                slab[t, gp, j * LANES : (j + 1) * LANES, :] = taken[t, :, j * 4 + gp, :].T
+                slab[t, gp, j * LANES : (j + 1) * LANES, :] = turn(t, j * 4 + gp)
         store(t).start()
     for t in range(2):
         load(8 + t).wait()
         for half in range(2):
             for yb in range(4):
-                peak[t, yb * LANES : (yb + 1) * LANES, half * LANES : (half + 1) * LANES] = (
-                    taken[8 + t, :, half * 4 + yb, :].T
+                peak[t, yb * LANES : (yb + 1) * LANES, half * LANES : (half + 1) * LANES] = turn(
+                    8 + t, half * 4 + yb
                 )
         store_peak(t).start()
     for t in range(8):
@@ -387,6 +394,7 @@
             pltpu.SemaphoreType.DMA((2,)),
         ],
         name="unpack",
+        compiler_params=pltpu.CompilerParams(vmem_limit_bytes=16 << 20),
     )(arrived)
 
 
@@ -399,11 +407,12 @@
     starts = jnp.cumsum(y_sizes) - y_sizes
     matrices = tuple(jnp.asarray(part) for part in spectral_pair())
     order = lane_order(new_col)
+    first_row = old_place * CAP
     pair = exchange(pack_pair(velocity))
     derived = exchange(pack_derived(velocity, matrices))
-    part = slope_z(gather(pair, 0, starts, old_place, "gather_2"), matrices)
-    part = slope_y(gather(pair, 1, starts, old_place, "gather_1"), matrices, part)
-    packed = finish(derived, part, order, starts, old_place)
+    part = slope_z(gather(pair, 0, starts, first_row, "gather_2"), matrices)
+    part = slope_y(gather(pair, 1, starts, first_row, "gather_1"), matrices, part)
+    packed = finish(derived, part, order, starts, first_row)
     slab, peak = unpack(exchange(packed.reshape(DEVICES, PLACED, LANES)))
     return slab.reshape(2, 1, 2, N, N), peak
 

time: 295 us -> 284 us (0.963)
  Pallas kernels: 79.7 us -> 60.4 us
  waiting for transfers between devices: 124 us -> 132 us
    all_to_all x2, waiting for transfers between devices: 124 us -> 132 us  [exchange(): return lax.all_to_all(value, AXES, split_axis=0, concat_axis=0, tiled=True)]
    pallas_call x2, Pallas kernels: 21.8 us -> 14 us  [gather(): pl.pallas_call(gather_kernel, grid_spec=pltpu.PrefetchScalarGridSpec(num_...]
    pallas_call x1, Pallas kernels: 17.1 us -> 9.67 us  [finish(): pl.pallas_call(finish_kernel, grid_spec=pltpu.PrefetchScalarGridSpec(num_...]
  transfers between devices with their start and end apart: 2 -> 2, of which waited for: 2 -> 2; matrix products, arithmetic and copies ran while one was open for 1% -> 1% of each run, Pallas kernels for 16% -> 14%
where the time goes in v3:
time: 284 us; the launch traced here: 283 us
  waiting for transfers between devices  132 us (46%)
  blocking collectives  69.8 us (25%)
  Pallas kernels  60.4 us (21%)
  starting transfers between devices  17.7 us (6%)
    all_to_all x2, waiting for transfers between devices, exchange(): return lax.all_to_all(value, AXES, split_axis=0, concat_axis=0, tiled=True)  132 us
    all_to_all x1, blocking collectives, exchange(): return lax.all_to_all(value, AXES, split_axis=0, concat_axis=0, tiled=True)  69.8 us
    all_to_all x2, starting transfers between devices, exchange(): return lax.all_to_all(value, AXES, split_axis=0, concat_axis=0, tiled=True)  17.7 us
    pallas_call x2, Pallas kernels, gather(): pl.pallas_call(gather_kernel, grid_spec=pltpu.PrefetchScalarGridSpec(num_...  14 us
    pallas_call x1, Pallas kernels, pack_derived(): pl.pallas_call(pack_slope, grid=(STEPS,), in_specs=[pl.BlockSpec((1, 8, Z...  10.8 us
    pallas_call x1, Pallas kernels, finish(): pl.pallas_call(finish_kernel, grid_spec=pltpu.PrefetchScalarGridSpec(num_...  9.67 us
    pallas_call x1, Pallas kernels, slope_y(): pl.pallas_call(slope_y_kernel, grid=(KX,), in_specs=[BLOCK, WHOLE, WHOLE,...  7.97 us
    pallas_call x1, Pallas kernels, pack_pair(): pl.pallas_call(pack_pair_kernel, in_specs=[pl.BlockSpec(memory_space=pltp...  7.36 us
  transfers between devices with their start and end apart: 2, of which 2 were waited for; matrix products, arithmetic and copies ran while one was open for 1% of the time, Pallas kernels for 14%

profile of v3, /device:TPU:0, one launch (start us, length us, event | category | flops | bytes accessed | tf_op | source)
XLA Modules:
  0.0 283.2 jit_solution(4240328302918047854)
XLA Ops:
  0.6 7.4 %pack_pair.1 = f32[128,144,128]{2,1,0:T(8,128)} custom-call(f32[3,72,32,512]{3,2,1,0:T(8,128)} %bitcast.11), custom_call_target="tpu_custom_call" | custom-call | flops 1207959552 | bytes 18874368 | tf_op jit(solution)/shard_map/pack_pair/pallas_call | solution.py:82
  8.0 11.6 %all-to-all-start.1 = ((f32[128,144,128]{2,1,0:T(8,128)}), f32[128,144,128]{2,1,0:T(8,128)}, u32[]{:S(2)}, u32[]{:S(2)}) async-start(f32[128,144,128]{2,1,0:T(8,128)} %pack_pair.1), calls=%async_computation.1 | async-start | bytes 18874368 | tf_op jit(solution)/shard_map/all_to_all | solution.py:402
  19.6 10.8 %pack_slope.1 = f32[128,72,128]{2,1,0:T(8,128)} custom-call(f32[3,72,32,512]{3,2,1,0:T(8,128)} %bitcast.12, bf16[512,512]{1,0:T(8,128)(2,1)} %constant.17.clone.high_ref, bf16[512,512]{1,0:T(8,128)(2,1)} %constant.18.clone.low_ref), custom_call_target="tpu_custom_call" | custom-call | flops 3623878656 | bytes 9437184 | tf_op jit(solution)/shard_map/pack_slope/pallas_call | solution.py:108
  30.5 106.0 %all-to-all-done.1 = f32[128,144,128]{2,1,0:T(8,128)} async-done(((f32[128,144,128]{2,1,0:T(8,128)}), f32[128,144,128]{2,1,0:T(8,128)}, u32[]{:S(2)}, u32[]{:S(2)}) %all-to-all-start.1) | async-done | bytes 9437216 | tf_op jit(solution)/shard_map/all_to_all | solution.py:402
  136.5 6.0 %all-to-all-start = ((f32[128,72,128]{2,1,0:T(8,128)}), f32[128,72,128]{2,1,0:T(8,128)}, u32[]{:S(2)}, u32[]{:S(2)}) async-start(f32[128,72,128]{2,1,0:T(8,128)} %pack_slope.1), calls=%async_computation | async-start | bytes 9437184 | tf_op jit(solution)/shard_map/all_to_all | solution.py:402
  142.5 0.0 copy-done.2
  142.5 0.1 copy.13
  142.6 0.1 reduce
  142.8 0.5 sub.3.starts
  143.3 0.0 copy-done
  143.3 0.1 select_reduce_fusion
  143.4 0.1 add_bitcast_fusion
  143.5 0.1 add.37
  143.6 0.1 add.39
  143.7 0.6 broadcast_add_fusion.order_ref
  144.3 0.6 broadcast_multiply_fusion.1.places
  144.9 7.0 %gather_2.1.field_ref = f32[4,512,512]{2,1,0:T(8,128)} custom-call(s32[16]{0:T(128)} %sub.3.starts, s32[16,16]{1,0:T(8,128)} %broadcast_multiply_fusion.1.places, f32[16,8,144,128]{3,2,1,0:T(8,128)} %bitcast.5.in_ref), custom_call_target="tpu_custom_call" | custom-call | flops 1073741824 | bytes 8388608 | tf_op jit(solution)/shard_map/gather_2/pallas_call | solution.py:166
  151.9 7.0 %gather_1.1.field_ref = f32[4,512,512]{2,1,0:T(8,128)} custom-call(s32[16]{0:T(128)} %sub.3.starts, s32[16,16]{1,0:T(8,128)} %broadcast_multiply_fusion.1.places, f32[16,8,144,128]{3,2,1,0:T(8,128)} %bitcast.5.in_ref), custom_call_target="tpu_custom_call" | custom-call | flops 1073741824 | bytes 8388608 | tf_op jit(solution)/shard_map/gather_1/pallas_call | solution.py:166
  158.9 7.2 %slope_z.1.add_ref = f32[4,512,512]{2,1,0:T(8,128)} custom-call(f32[4,512,512]{2,1,0:T(8,128)} %gather_2.1.field_ref, bf16[512,512]{1,0:T(8,128)(2,1)} %constant.17.clone.high_ref, bf16[512,512]{1,0:T(8,128)(2,1)} %constant.18.clone.low_ref), custom_call_target="tpu_custom_call" | custom-call | flops 3221225472 | bytes 8388608 | tf_op jit(solution)/shard_map/slope_z/pallas_call | solution.py:201
  166.1 8.0 %slope_y.1.part_ref = f32[4,4,512,128]{3,2,1,0:T(8,128)} custom-call(f32[4,512,512]{2,1,0:T(8,128)} %gather_1.1.field_ref, bf16[512,512]{1,0:T(8,128)(2,1)} %constant.17.clone.high_ref, bf16[512,512]{1,0:T(8,128)(2,1)} %constant.18.clone.low_ref, f32[4,512,512]{2,1,0:T(8,128)} %slope_z.1.add_ref), custom_call_target="tpu_custom_call" | custom-call | flops 3221225472 | bytes 8388608 | tf_op jit(solution)/shard_map/slope_y/pallas_call | solution.py:213
  174.0 26.2 %all-to-all-done = f32[128,72,128]{2,1,0:T(8,128)} async-done(((f32[128,72,128]{2,1,0:T(8,128)}), f32[128,72,128]{2,1,0:T(8,128)}, u32[]{:S(2)}, u32[]{:S(2)}) %all-to-all-start) | async-done | bytes 4718624 | tf_op jit(solution)/shard_map/all_to_all | solution.py:402
  200.2 9.7 %finish.1 = f32[16,8,80,128]{3,2,1,0:T(8,128)} custom-call(s32[16]{0:T(128)} %sub.3.starts, s32[16,16]{1,0:T(8,128)} %broadcast_multiply_fusion.1.places, s32[4,128]{1,0:T(4,128)} %broadcast_add_fusion.order_ref, f32[16,8,72,128]{3,2,1,0:T(8,128)} %bitcast.4.in_ref, f32[4,4,512,128]{3,2,1,0:T(8,128)} %slope_y.1.part_ref), custom_call_target="tpu_custom_call" | custom-call | flops 536870912 | bytes 16777216 | tf_op jit(solution)/shard_map/finish/pallas_call | solution.py:293
  209.9 69.8 %all_to_all.15.in_ref = f32[128,80,128]{2,1,0:T(8,128)S(1)} all-to-all(f32[128,80,128]{2,1,0:T(8,128)} %bitcast.13), channel_id=1, replica_groups=mesh['row'=8,'col'=16] {'col','row'}, dimensions={0} | all-to-all | bytes 10485760 | tf_op jit(solution)/shard_map/all_to_all | solution.py:402
  279.7 3.4 %unpack.1 = (f32[4,512,512]{2,1,0:T(8,128)}, f32[512,512]{1,0:T(8,128)}) custom-call(f32[128,80,128]{2,1,0:T(8,128)S(1)} %all_to_all.15.in_ref), custom_call_target="tpu_custom_call" | custom-call | tf_op jit(solution)/shard_map/unpack/pallas_call | solution.py:380
  (10 shorter events, 0.1 us)
Async XLA Ops:
  8.0 128.5 %all-to-all-start.1 = ((f32[128,144,128]{2,1,0:T(8,128)}), f32[128,144,128]{2,1,0:T(8,128)}, u32[]{:S(2)}, u32[]{:S(2)}) async-start(f32[128,144,128]{2,1,0:T(8,128)} %pack_pair.1), calls=%async_computation.1 | async-start | bytes 18874368 | tf_op jit(solution)/shard_map/all_to_all | solution.py:402
  30.5 112.0 %copy-start.2 = (s32[16]{0:T(128)S(1)}, s32[16]{0:T(128)}, u32[]{:S(2)}) copy-start(s32[16]{0:T(128)} %param.7) | copy-start | bytes 196
  30.5 112.8 %copy-start = (s32[16,16]{1,0:T(8,128)S(1)}, s32[16,16]{1,0:T(8,128)}, u32[]{:S(2)}) copy-start(s32[16,16]{1,0:T(8,128)} %param.9) | copy-start | bytes 3076
  30.5 113.8 %copy-start.1 = (s32[16,16]{1,0:T(8,128)S(1)}, s32[16,16]{1,0:T(8,128)}, u32[]{:S(2)}) copy-start(s32[16,16]{1,0:T(8,128)} %param.8) | copy-start | bytes 3076
  136.5 63.7 %all-to-all-start = ((f32[128,72,128]{2,1,0:T(8,128)}), f32[128,72,128]{2,1,0:T(8,128)}, u32[]{:S(2)}, u32[]{:S(2)}) async-start(f32[128,72,128]{2,1,0:T(8,128)} %pack_slope.1), calls=%async_computation | async-start | bytes 9437184 | tf_op jit(solution)/shard_map/all_to_all | solution.py:402

commit v4 on v3

v4 whole, which is shorter than its diff:
```python
import jax
import jax.numpy as jnp
import numpy as np
from jax import lax
from jax.experimental import pallas as pl
from jax.experimental.pallas import tpu as pltpu
from jax.sharding import PartitionSpec as P

AXES = ("col", "row")
LANES = 128
N = 512
DEVICES = 128
KX = N // DEVICES
ROWS = 72
CAP = 36
SENT = 3 * ROWS
PLACED = 80
ZB = 32
NB = 16
NR = 8
PACK_MIB = 44
MIDDLE_MIB = 26


def spectral_pair():
    gap = (np.arange(N)[:, None] - np.arange(N)[None, :]) % N
    angle = gap * (np.pi / N)
    parity = 1.0 - 2.0 * (gap % 2)
    safe = np.where(gap == 0, 1.0, np.sin(angle))
    full = np.where(gap == 0, 0.0, parity * np.cos(angle) / safe * (2.0 / N))
    full = (full - full.T) / 2
    high = full.astype(jnp.bfloat16)
    low = (full - high.astype(np.float64)).astype(jnp.bfloat16)
    return high, low


def halves(value):
    high = value.astype(jnp.bfloat16)
    return high, (value - high.astype(jnp.float32)).astype(jnp.bfloat16)


def mul(left, right):
    return jnp.dot(left, right, preferred_element_type=jnp.float32)


def mul3(left, right):
    return mul(left[0], right[0]) + (mul(left[1], right[0]) + mul(left[0], right[1]))


def pack_row(value, flat, row):
    tall = jnp.concatenate([value[:, k * LANES : (k + 1) * LANES] for k in range(KX)], axis=0)
    flat[pl.ds(row, DEVICES, stride=SENT), :] = tall.T


FIELDS = (2, 1, 0)
STEPS = ROWS // 8


def pack_kernel(in_ref, high_ref, low_ref, out_ref, taken, high, low, in_sem, sem):
    flat = out_ref.reshape(DEVICES * SENT, LANES)

    def load(step):
        field, t = divmod(step, STEPS)
        return pltpu.make_async_copy(
            in_ref.at[FIELDS[field], pl.ds(t * 8, 8)], taken.at[step], in_sem.at[step]
        )

    constants = (
        pltpu.make_async_copy(high_ref, high, sem.at[0]),
        pltpu.make_async_copy(low_ref, low, sem.at[1]),
    )
    for step in range(3 * STEPS):
        load(step).start()
        if step == STEPS:
            for copy in constants:
                copy.start()
    for copy in constants:
        copy.wait()
    for step in range(3 * STEPS):
        load(step).wait()
        value = taken[step].reshape(8 * ZB, N)
        if FIELDS[step // STEPS] == 0:
            value = -mul3(halves(value), (high[...], low[...]))
        for i in range(8):
            pack_row(value[i * ZB : (i + 1) * ZB], flat, step * 8 + i)


def pack(velocity, matrices):
    far = pl.BlockSpec(memory_space=pltpu.HBM)
    return pl.pallas_call(
        pack_kernel,
        in_specs=[far, far, far],
        out_specs=pl.BlockSpec(memory_space=pltpu.VMEM),
        out_shape=pltpu.VMEM((DEVICES, SENT, LANES), jnp.float32),
        scratch_shapes=[
            pltpu.VMEM((3 * STEPS, 8, ZB, N), jnp.float32),
            pltpu.VMEM((N, N), jnp.bfloat16),
            pltpu.VMEM((N, N), jnp.bfloat16),
            pltpu.SemaphoreType.DMA((3 * STEPS,)),
            pltpu.SemaphoreType.DMA((2,)),
        ],
        name="pack",
        compiler_params=pltpu.CompilerParams(vmem_limit_bytes=PACK_MIB << 20),
    )(velocity, *matrices)


def turn_lanes(parts):
    lane = lax.broadcasted_iota(jnp.int32, parts[0].shape, 1)
    upper = (lane // 64) == 1
    odd = (lane // 32) % 2 == 1
    a0, a1, a2, a3 = parts
    b0 = jnp.where(upper, pltpu.roll(a2, 64, 1), a0)
    b2 = jnp.where(upper, a2, pltpu.roll(a0, 64, 1))
    b1 = jnp.where(upper, pltpu.roll(a3, 64, 1), a1)
    b3 = jnp.where(upper, a3, pltpu.roll(a1, 64, 1))
    c0 = jnp.where(odd, pltpu.roll(b1, 32, 1), b0)
    c1 = jnp.where(odd, b1, pltpu.roll(b0, 96, 1))
    c2 = jnp.where(odd, pltpu.roll(b3, 32, 1), b2)
    c3 = jnp.where(odd, b3, pltpu.roll(b2, 96, 1))
    return c0, c1, c2, c3


LINED = 560
MADE = 72


def middle_kernel(
    sizes, places, columns, high_ref, low_ref, in_ref, out_ref,
    starts, first, high, low, lined, field_high, field_low, part, total, made, top, spread,
    sem, out_sem, peak_sem,
):
    constants = (
        pltpu.make_async_copy(high_ref, high, sem.at[0]),
        pltpu.make_async_copy(low_ref, low, sem.at[1]),
    )
    for copy in constants:
        copy.start()

    start = jnp.int32(0)
    for b in range(NB):
        starts[b] = start
        start = start + sizes[b]

    def rows_of(c, carry):
        for b in range(NB):
            place = places[c, b]
            first[c, b] = place * CAP + (place >> 1) * (SENT - ROWS)
        return carry

    lax.fori_loop(0, NB, rows_of, 0)
    flat = in_ref.reshape(NB, NR * SENT, LANES)

    def quad_of(field, quad):
        for cc in range(4):
            for b in range(NB):
                row = first[quad * 4 + cc, b] + field * ROWS
                lined[cc, pl.ds(starts[b], CAP), :] = flat[quad * 4 + cc, pl.ds(row, CAP), :]
        return turn_lanes([lined[cc, 0:N, :] for cc in range(4)])

    def store(quad, side):
        return pltpu.make_async_copy(
            made.at[quad, pl.ds(side * NB, NB), pl.ds(0, 64), :],
            out_ref.at[:, quad * 2 + side, pl.ds(0, 64), :],
            out_sem.at[quad, side],
        )

    def split_z(quad, carry):
        turned = quad_of(0, quad)
        for k in range(KX):
            field_high[k, quad], field_low[k, quad] = halves(turned[k])
        return carry

    lax.fori_loop(0, 4, split_z, 0)
    for copy in constants:
        copy.wait()

    def slope_z(k, carry):
        left = [
            jnp.concatenate([ref[k, quad] for quad in range(4)], axis=1)
            for ref in (field_high, field_low)
        ]
        slope = mul3(left, (high[...], low[...]))
        for quad in range(4):
            part[quad, k] = -slope[:, quad * LANES : (quad + 1) * LANES]
        return carry

    lax.fori_loop(0, KX, slope_z, 0)
    top[...] = jnp.zeros_like(top)
    lane = lax.broadcasted_iota(jnp.int32, (8, LANES), 1)
    lane_block = ((lane // NB) % 2) * 2 + lane // 64
    lane_column = lane % NB

    def one(quad, carry):
        wide = jnp.concatenate(quad_of(1, quad), axis=1)
        slope = mul3((high[...], low[...]), halves(wide))
        for k in range(KX):
            part[quad, k] = part[quad, k] + slope[:, k * LANES : (k + 1) * LANES]
        order = lane_block * ZB + (lane // 32) % 2
        for cc in range(4):
            for slab in range(NB):
                hit = (lane_block == cc) & (lane_column == columns[quad * 4 + cc, slab])
                order = order + jnp.where(hit, 2 * slab, 0)
        order = jnp.concatenate([order] * (N // 8), axis=0)
        turned = quad_of(2, quad)
        for k in range(KX):
            value = turned[k] + part[quad, k]
            total[k] = jnp.take_along_axis(value, order, axis=1)
        for k in range(KX):
            for yb in range(4):
                tile = total[k, yb * LANES : (yb + 1) * LANES, :].T
                at = k * 4 + yb
                rows = made.at[quad].reshape(32 * MADE, LANES)
                for gp in range(4):
                    rows[pl.ds(at * 4 + gp, 32, stride=MADE), :] = tile[gp * 32 : (gp + 1) * 32, :]
                best = jnp.max(jnp.abs(tile).reshape(16, 8, LANES), axis=0)
                top[at * 8 : at * 8 + 8, :] = jnp.maximum(top[at * 8 : at * 8 + 8, :], best)
        for side in range(2):
            store(quad, side).start()
        return carry

    lax.fori_loop(0, 4, one, 0)
    peak = jnp.max(top[...].reshape(16, 8, LANES), axis=1)
    spread[...] = jnp.broadcast_to(peak[None, None], spread.shape)
    last = pltpu.make_async_copy(spread, out_ref.at[:, :, pl.ds(64, 16), :], peak_sem)
    last.start()
    for quad in range(4):
        for side in range(2):
            store(quad, side).wait()
    last.wait()


def middle(received, matrices, y_sizes, old_place, new_col):
    anywhere = pl.BlockSpec(memory_space=pl.ANY)
    far = pl.BlockSpec(memory_space=pltpu.HBM)
    near = pl.BlockSpec(memory_space=pltpu.SMEM)
    return pl.pallas_call(
        middle_kernel,
        in_specs=[near, near, near, far, far, pl.BlockSpec(memory_space=pltpu.VMEM)],
        out_specs=anywhere,
        out_shape=pltpu.VMEM((NB, NR, PLACED, LANES), jnp.float32),
        scratch_shapes=[
            pltpu.SMEM((NB,), jnp.int32),
            pltpu.SMEM((NB, NB), jnp.int32),
            pltpu.VMEM((N, N), jnp.bfloat16),
            pltpu.VMEM((N, N), jnp.bfloat16),
            pltpu.VMEM((4, LINED, LANES), jnp.float32),
            pltpu.VMEM((KX, 4, N, LANES), jnp.bfloat16),
            pltpu.VMEM((KX, 4, N, LANES), jnp.bfloat16),
            pltpu.VMEM((4, KX, N, LANES), jnp.float32),
            pltpu.VMEM((KX, N, LANES), jnp.float32),
            pltpu.VMEM((4, 32, MADE, LANES), jnp.float32),
            pltpu.VMEM((LANES, LANES), jnp.float32),
            pltpu.VMEM((NB, NR, 16, LANES), jnp.float32),
            pltpu.SemaphoreType.DMA((2,)),
            pltpu.SemaphoreType.DMA((4, 2)),
            pltpu.SemaphoreType.DMA,
        ],
        name="middle",
        compiler_params=pltpu.CompilerParams(vmem_limit_bytes=MIDDLE_MIB << 20),
    )(y_sizes, old_place, new_col, *matrices, received.reshape(NB, NR, SENT, LANES))


def unpack_kernel(in_ref, slab_ref, peak_ref, taken, slab, peak, in_sem, slab_sem, peak_sem):
    def load(t):
        return pltpu.make_async_copy(
            in_ref.at[:, pl.ds(t * 8, 8), :], taken.at[t], in_sem.at[t]
        )

    def store(t):
        k, m = divmod(t, 2)
        return pltpu.make_async_copy(
            slab.at[t],
            slab_ref.at[:, pl.ds(m * 256, 256), pl.ds(k * LANES, LANES)],
            slab_sem.at[t],
        )

    def store_peak(t):
        return pltpu.make_async_copy(
            peak.at[t], peak_ref.at[:, pl.ds(t * 256, 256)], peak_sem.at[t]
        )

    def turn(t, row):
        flat = taken.at[t].reshape(DEVICES * 8, LANES)
        return flat[pl.ds(row, DEVICES, stride=8), :].T

    for t in range(10):
        load(t).start()
    for t in range(8):
        load(t).wait()
        for j in range(2):
            for gp in range(4):
                slab[t, gp, j * LANES : (j + 1) * LANES, :] = turn(t, j * 4 + gp)
        store(t).start()
    for t in range(2):
        load(8 + t).wait()
        for half in range(2):
            for yb in range(4):
                peak[t, yb * LANES : (yb + 1) * LANES, half * LANES : (half + 1) * LANES] = turn(
                    8 + t, half * 4 + yb
                )
        store_peak(t).start()
    for t in range(8):
        store(t).wait()
    for t in range(2):
        store_peak(t).wait()


def unpack(arrived):
    anywhere = pl.BlockSpec(memory_space=pl.ANY)
    return pl.pallas_call(
        unpack_kernel,
        in_specs=[anywhere],
        out_specs=[anywhere, anywhere],
        out_shape=[
            jax.ShapeDtypeStruct((4, N, N), jnp.float32),
            jax.ShapeDtypeStruct((N, N), jnp.float32),
        ],
        scratch_shapes=[
            pltpu.VMEM((10, DEVICES, 8, LANES), jnp.float32),
            pltpu.VMEM((8, 4, 256, LANES), jnp.float32),
            pltpu.VMEM((2, N, 256), jnp.float32),
            pltpu.SemaphoreType.DMA((10,)),
            pltpu.SemaphoreType.DMA((8,)),
            pltpu.SemaphoreType.DMA((2,)),
        ],
        name="unpack",
        compiler_params=pltpu.CompilerParams(vmem_limit_bytes=16 << 20),
    )(arrived)


def exchange(value):
    return lax.all_to_all(value, AXES, split_axis=0, concat_axis=0, tiled=True)


def on_device(velocity, y_sizes, old_place, new_col):
    matrices = tuple(jnp.asarray(part) for part in spectral_pair())
    received = exchange(pack(velocity.reshape(3, ROWS, ZB, N), matrices))
    packed = middle(received, matrices, y_sizes, old_place, new_col)
    slab, peak = unpack(exchange(packed.reshape(DEVICES, PLACED, LANES)))
    return slab.reshape(2, 1, 2, N, N), peak


def solution(mesh):
    in_specs = (P(None, "col", "row", None, None, None), P(), P(), P())
    out_specs = (P("row", "col", None, None, None), P())
    return jax.shard_map(
        on_device, mesh=mesh, in_specs=in_specs, out_specs=out_specs, check_vma=False
    )
```

time: 284 us -> 278 us (0.979)
  blocking collectives: 69.8 us -> 241 us
  waiting for transfers between devices: 132 us -> 0 us
  Pallas kernels: 60.4 us -> 36.8 us
  starting transfers between devices: 17.7 us -> 0 us
    all_to_all x1 -> x2, blocking collectives: 69.8 us -> 241 us  [exchange(): return lax.all_to_all(value, AXES, split_axis=0, concat_axis=0, tiled=True)]
    all_to_all x2 -> x0, waiting for transfers between devices: 132 us -> none  [exchange(): return lax.all_to_all(value, AXES, split_axis=0, concat_axis=0, tiled=True)]
    pallas_call x7 -> x2, Pallas kernels: 57 us -> 33.4 us  [the longest x1 17.9 us: middle(): pl.pallas_call(middle_kernel, in_specs=[near, near, near, far, far, pl.Bl...]
    all_to_all x2 -> x0, starting transfers between devices: 17.7 us -> none  [exchange(): return lax.all_to_all(value, AXES, split_axis=0, concat_axis=0, tiled=True)]
  transfers between devices with their start and end apart: 2 -> 0, of which waited for: 2 -> 0; matrix products, arithmetic and copies ran while one was open for 1% -> 0% of each run, Pallas kernels for 14% -> 0%
where the time goes in v4:
time: 278 us
  blocking collectives  241 us (87%)
  Pallas kernels  36.8 us (13%)
    all_to_all x2, blocking collectives, exchange(): return lax.all_to_all(value, AXES, split_axis=0, concat_axis=0, tiled=True)  241 us
    pallas_call x1, Pallas kernels, middle(): pl.pallas_call(middle_kernel, in_specs=[near, near, near, far, far, pl.Bl...  17.9 us
    pallas_call x1, Pallas kernels, pack(): pl.pallas_call(pack_kernel, in_specs=[far, far, far], out_specs=pl.BlockS...  15.5 us

profile of v4, /device:TPU:0, one launch (start us, length us, event | category | flops | bytes accessed | tf_op | source)
XLA Modules:
  0.0 278.3 jit_solution(11063948548140480839)
XLA Ops:
  0.6 15.5 %pack.1 = f32[128,216,128]{2,1,0:T(8,128)S(1)} custom-call(f32[3,72,32,512]{3,2,1,0:T(8,128)} %bitcast.8, bf16[512,512]{1,0:T(8,128)(2,1)} %constant.4.clone.high_ref, bf16[512,512]{1,0:T(8,128)(2,1)} %constant.5.clone.low_ref), custom_call_target="tpu_custom_call" | custom-call | tf_op jit(solution)/shard_map/pack/pallas_call | solution.py:90
  16.2 0.0 copy-start
  16.2 0.0 copy-start.1
  16.2 0.0 copy-start.2
  16.2 0.0 copy-start.3
  16.2 0.0 copy-start.4
  16.2 171.8 %all_to_all.10 = f32[128,216,128]{2,1,0:T(8,128)S(1)} all-to-all(f32[128,216,128]{2,1,0:T(8,128)S(1)} %pack.1), channel_id=1, replica_groups=mesh['row'=8,'col'=16] {'col','row'}, dimensions={0} | all-to-all | bytes 28311552 | tf_op jit(solution)/shard_map/all_to_all | solution.py:332
  188.0 0.0 copy-done
  188.0 0.0 copy-done.1
  188.0 0.0 copy-done.2
  188.0 0.0 copy-done.3
  188.0 0.0 copy-done.4
  188.0 17.9 %middle.1 = f32[16,8,80,128]{3,2,1,0:T(8,128)S(1)} custom-call(s32[16]{0:T(128)S(1)} %copy-done.4, s32[16,16]{1,0:T(8,128)S(1)} %copy-done.2, s32[16,16]{1,0:T(8,128)S(1)} %copy-done.3, bf16[512,512]{1,0:T(8,128)(2,1)S(1)} %copy-done.1, bf16[512,512]{1,0:T(8,128)(2,1)S(1)} %copy-done, f32[16,8,216,128]{3,2,1,0:T(8,128)S(1)} %bitcast.6), custom_call_target="tpu_custom_call" | custom-call | tf_op jit(solution)/shard_map/middle/pallas_call | solution.py:236
  205.9 68.8 %all_to_all.11.in_ref = f32[128,80,128]{2,1,0:T(8,128)S(1)} all-to-all(f32[128,80,128]{2,1,0:T(8,128)S(1)} %bitcast.7), channel_id=1, replica_groups=mesh['row'=8,'col'=16] {'col','row'}, dimensions={0} | all-to-all | bytes 10485760 | tf_op jit(solution)/shard_map/all_to_all | solution.py:332
  274.8 3.4 %unpack.1 = (f32[4,512,512]{2,1,0:T(8,128)}, f32[512,512]{1,0:T(8,128)}) custom-call(f32[128,80,128]{2,1,0:T(8,128)S(1)} %all_to_all.11.in_ref), custom_call_target="tpu_custom_call" | custom-call | tf_op jit(solution)/shard_map/unpack/pallas_call | solution.py:310
Async XLA Ops:
  16.2 171.8 %copy-start = (bf16[512,512]{1,0:T(8,128)(2,1)S(1)}, bf16[512,512]{1,0:T(8,128)(2,1)}, u32[]{:S(2)}) copy-start(bf16[512,512]{1,0:T(8,128)(2,1)} %constant.5.clone.low_ref) | copy-start | bytes 1572868
  16.2 171.8 %copy-start.1 = (bf16[512,512]{1,0:T(8,128)(2,1)S(1)}, bf16[512,512]{1,0:T(8,128)(2,1)}, u32[]{:S(2)}) copy-start(bf16[512,512]{1,0:T(8,128)(2,1)} %constant.4.clone.high_ref) | copy-start | bytes 1572868
  16.2 171.8 %copy-start.2 = (s32[16,16]{1,0:T(8,128)S(1)}, s32[16,16]{1,0:T(8,128)}, u32[]{:S(2)}) copy-start(s32[16,16]{1,0:T(8,128)} %places.1) | copy-start | bytes 3076
  16.2 171.8 %copy-start.3 = (s32[16,16]{1,0:T(8,128)S(1)}, s32[16,16]{1,0:T(8,128)}, u32[]{:S(2)}) copy-start(s32[16,16]{1,0:T(8,128)} %columns.1) | copy-start | bytes 3076
  16.2 171.8 %copy-start.4 = (s32[16]{0:T(128)S(1)}, s32[16]{0:T(128)}, u32[]{:S(2)}) copy-start(s32[16]{0:T(128)} %sizes.1) | copy-start | bytes 196

commit v5 on v4

--- a/solution.py
+++ b/solution.py
@@ -9,6 +9,7 @@
 AXES = ("col", "row")
 LANES = 128
 N = 512
+HALF = N // 2
 DEVICES = 128
 KX = N // DEVICES
 ROWS = 72
@@ -29,8 +30,10 @@
     safe = np.where(gap == 0, 1.0, np.sin(angle))
     full = np.where(gap == 0, 0.0, parity * np.cos(angle) / safe * (2.0 / N))
     full = (full - full.T) / 2
-    high = full.astype(jnp.bfloat16)
-    low = (full - high.astype(np.float64)).astype(jnp.bfloat16)
+    first, second = full[:HALF, :HALF], full[:HALF, HALF:]
+    both = np.concatenate([(first + second) / 2, (first - second) / 2], axis=0)
+    high = both.astype(jnp.bfloat16)
+    low = (both - high.astype(np.float64)).astype(jnp.bfloat16)
     return high, low
 
 
@@ -47,6 +50,26 @@
     return mul(left[0], right[0]) + (mul(left[1], right[0]) + mul(left[0], right[1]))
 
 
+def parts_of(high, low):
+    return (high[:HALF], low[:HALF]), (high[HALF:], low[HALF:])
+
+
+def derive_lanes(value, high, low):
+    even, odd = parts_of(high, low)
+    left, right = value[:, :HALF], value[:, HALF:]
+    from_sum = mul3(halves(left + right), even)
+    from_difference = mul3(halves(left - right), odd)
+    return jnp.concatenate([-(from_sum + from_difference), from_difference - from_sum], axis=1)
+
+
+def derive_rows(value, high, low):
+    even, odd = parts_of(high, low)
+    top, bottom = value[:HALF], value[HALF:]
+    from_sum = mul3(even, halves(top + bottom))
+    from_difference = mul3(odd, halves(top - bottom))
+    return jnp.concatenate([from_sum + from_difference, from_sum - from_difference], axis=0)
+
+
 def pack_row(value, flat, row):
     tall = jnp.concatenate([value[:, k * LANES : (k + 1) * LANES] for k in range(KX)], axis=0)
     flat[pl.ds(row, DEVICES, stride=SENT), :] = tall.T
@@ -54,6 +77,7 @@
 
 FIELDS = (2, 1, 0)
 STEPS = ROWS // 8
+GROUP = 3
 
 
 def pack_kernel(in_ref, high_ref, low_ref, out_ref, taken, high, low, in_sem, sem):
@@ -71,18 +95,21 @@
     )
     for step in range(3 * STEPS):
         load(step).start()
-        if step == STEPS:
-            for copy in constants:
-                copy.start()
+    for copy in constants:
+        copy.start()
+    for step in range(2 * STEPS):
+        load(step).wait()
+        for i in range(8):
+            pack_row(taken[step, i], flat, step * 8 + i)
     for copy in constants:
         copy.wait()
-    for step in range(3 * STEPS):
-        load(step).wait()
-        value = taken[step].reshape(8 * ZB, N)
-        if FIELDS[step // STEPS] == 0:
-            value = -mul3(halves(value), (high[...], low[...]))
-        for i in range(8):
-            pack_row(value[i * ZB : (i + 1) * ZB], flat, step * 8 + i)
+    for group in range(2 * STEPS, 3 * STEPS, GROUP):
+        for step in range(group, group + GROUP):
+            load(step).wait()
+        lines = taken[group : group + GROUP].reshape(GROUP * 8 * ZB, N)
+        slope = derive_lanes(lines, high[...], low[...])
+        for i in range(GROUP * 8):
+            pack_row(slope[i * ZB : (i + 1) * ZB], flat, group * 8 + i)
 
 
 def pack(velocity, matrices):
@@ -94,8 +121,8 @@
         out_shape=pltpu.VMEM((DEVICES, SENT, LANES), jnp.float32),
         scratch_shapes=[
             pltpu.VMEM((3 * STEPS, 8, ZB, N), jnp.float32),
-            pltpu.VMEM((N, N), jnp.bfloat16),
-            pltpu.VMEM((N, N), jnp.bfloat16),
+            pltpu.VMEM((N, HALF), jnp.bfloat16),
+            pltpu.VMEM((N, HALF), jnp.bfloat16),
             pltpu.SemaphoreType.DMA((3 * STEPS,)),
             pltpu.SemaphoreType.DMA((2,)),
         ],
@@ -121,12 +148,13 @@
 
 
 LINED = 560
+CHUNK = 128
 MADE = 72
 
 
 def middle_kernel(
     sizes, places, columns, high_ref, low_ref, in_ref, out_ref,
-    starts, first, high, low, lined, field_high, field_low, part, total, made, top, spread,
+    starts, first, high, low, lined, field, part, slope_y, total, made, top, spread,
     sem, out_sem, peak_sem,
 ):
     constants = (
@@ -150,12 +178,11 @@
     lax.fori_loop(0, NB, rows_of, 0)
     flat = in_ref.reshape(NB, NR * SENT, LANES)
 
-    def quad_of(field, quad):
+    def line_up(item, quad):
         for cc in range(4):
             for b in range(NB):
-                row = first[quad * 4 + cc, b] + field * ROWS
+                row = first[quad * 4 + cc, b] + item * ROWS
                 lined[cc, pl.ds(starts[b], CAP), :] = flat[quad * 4 + cc, pl.ds(row, CAP), :]
-        return turn_lanes([lined[cc, 0:N, :] for cc in range(4)])
 
     def store(quad, side):
         return pltpu.make_async_copy(
@@ -165,9 +192,10 @@
         )
 
     def split_z(quad, carry):
-        turned = quad_of(0, quad)
+        line_up(0, quad)
+        turned = turn_lanes([lined[cc, 0:N, :] for cc in range(4)])
         for k in range(KX):
-            field_high[k, quad], field_low[k, quad] = halves(turned[k])
+            field[k, quad] = turned[k]
         return carry
 
     lax.fori_loop(0, 4, split_z, 0)
@@ -175,13 +203,10 @@
         copy.wait()
 
     def slope_z(k, carry):
-        left = [
-            jnp.concatenate([ref[k, quad] for quad in range(4)], axis=1)
-            for ref in (field_high, field_low)
-        ]
-        slope = mul3(left, (high[...], low[...]))
+        line = jnp.concatenate([field[k, quad] for quad in range(4)], axis=1)
+        slope = derive_lanes(line, high[...], low[...])
         for quad in range(4):
-            part[quad, k] = -slope[:, quad * LANES : (quad + 1) * LANES]
+            part[quad, k] = slope[:, quad * LANES : (quad + 1) * LANES]
         return carry
 
     lax.fori_loop(0, KX, slope_z, 0)
@@ -191,20 +216,24 @@
     lane_column = lane % NB
 
     def one(quad, carry):
-        wide = jnp.concatenate(quad_of(1, quad), axis=1)
-        slope = mul3((high[...], low[...]), halves(wide))
-        for k in range(KX):
-            part[quad, k] = part[quad, k] + slope[:, k * LANES : (k + 1) * LANES]
+        line_up(1, quad)
+        wide = jnp.concatenate([lined[cc, 0:N, :] for cc in range(4)], axis=1)
+        slope = derive_rows(wide, high[...], low[...])
+        for cc in range(4):
+            slope_y[cc] = slope[:, cc * LANES : (cc + 1) * LANES]
         order = lane_block * ZB + (lane // 32) % 2
         for cc in range(4):
             for slab in range(NB):
                 hit = (lane_block == cc) & (lane_column == columns[quad * 4 + cc, slab])
                 order = order + jnp.where(hit, 2 * slab, 0)
-        order = jnp.concatenate([order] * (N // 8), axis=0)
-        turned = quad_of(2, quad)
-        for k in range(KX):
-            value = turned[k] + part[quad, k]
-            total[k] = jnp.take_along_axis(value, order, axis=1)
+        order = jnp.concatenate([order] * (CHUNK // 8), axis=0)
+        line_up(2, quad)
+        for at in range(0, N, CHUNK):
+            rows = slice(at, at + CHUNK)
+            turned = turn_lanes([slope_y[cc, rows, :] + lined[cc, rows, :] for cc in range(4)])
+            for k in range(KX):
+                value = turned[k] + part[quad, k, rows, :]
+                total[k, rows, :] = jnp.take_along_axis(value, order, axis=1)
         for k in range(KX):
             for yb in range(4):
                 tile = total[k, yb * LANES : (yb + 1) * LANES, :].T
@@ -241,12 +270,12 @@
         scratch_shapes=[
             pltpu.SMEM((NB,), jnp.int32),
             pltpu.SMEM((NB, NB), jnp.int32),
-            pltpu.VMEM((N, N), jnp.bfloat16),
-            pltpu.VMEM((N, N), jnp.bfloat16),
+            pltpu.VMEM((N, HALF), jnp.bfloat16),
+            pltpu.VMEM((N, HALF), jnp.bfloat16),
             pltpu.VMEM((4, LINED, LANES), jnp.float32),
-            pltpu.VMEM((KX, 4, N, LANES), jnp.bfloat16),
-            pltpu.VMEM((KX, 4, N, LANES), jnp.bfloat16),
+            pltpu.VMEM((KX, 4, N, LANES), jnp.float32),
             pltpu.VMEM((4, KX, N, LANES), jnp.float32),
+            pltpu.VMEM((4, N, LANES), jnp.float32),
             pltpu.VMEM((KX, N, LANES), jnp.float32),
             pltpu.VMEM((4, 32, MADE, LANES), jnp.float32),
             pltpu.VMEM((LANES, LANES), jnp.float32),

time: 278 us -> 269 us (0.968)
  Pallas kernels: 36.8 us -> 27.3 us
    pallas_call x1, Pallas kernels: 15.5 us -> 8.68 us  [pack(): pl.pallas_call(pack_kernel, in_specs=[far, far, far], out_specs=pl.BlockS...]
where the time goes in v5:
time: 269 us
  blocking collectives  241 us (90%)
  Pallas kernels  27.3 us (10%)
    all_to_all x2, blocking collectives, exchange(): return lax.all_to_all(value, AXES, split_axis=0, concat_axis=0, tiled=True)  241 us
    pallas_call x1, Pallas kernels, middle(): pl.pallas_call(middle_kernel, in_specs=[near, near, near, far, far, pl.Bl...  15.3 us
    pallas_call x1, Pallas kernels, pack(): pl.pallas_call(pack_kernel, in_specs=[far, far, far], out_specs=pl.BlockS...  8.68 us

profile of v5, /device:TPU:0, one launch (start us, length us, event | category | flops | bytes accessed | tf_op | source)
XLA Modules:
  0.0 268.8 jit_solution(5580349254108214388)
XLA Ops:
  0.6 8.7 %pack.1 = f32[128,216,128]{2,1,0:T(8,128)S(1)} custom-call(f32[3,72,32,512]{3,2,1,0:T(8,128)} %bitcast.8, bf16[512,256]{1,0:T(8,128)(2,1)} %constant.4.clone.high_ref, bf16[512,256]{1,0:T(8,128)(2,1)} %constant.5.clone.low_ref), custom_call_target="tpu_custom_call" | custom-call | tf_op jit(solution)/shard_map/pack/pallas_call | solution.py:117
  9.3 0.0 copy-start
  9.3 0.0 copy-start.1
  9.3 0.0 copy-start.2
  9.4 0.0 copy-start.3
  9.4 0.0 copy-start.4
  9.4 171.8 %all_to_all.10 = f32[128,216,128]{2,1,0:T(8,128)S(1)} all-to-all(f32[128,216,128]{2,1,0:T(8,128)S(1)} %pack.1), channel_id=1, replica_groups=mesh['row'=8,'col'=16] {'col','row'}, dimensions={0} | all-to-all | bytes 28311552 | tf_op jit(solution)/shard_map/all_to_all | solution.py:361
  181.1 0.0 copy-done
  181.2 0.0 copy-done.1
  181.2 0.0 copy-done.2
  181.2 0.0 copy-done.3
  181.2 0.0 copy-done.4
  181.2 15.3 %middle.1 = f32[16,8,80,128]{3,2,1,0:T(8,128)S(1)} custom-call(s32[16]{0:T(128)S(1)} %copy-done.4, s32[16,16]{1,0:T(8,128)S(1)} %copy-done.2, s32[16,16]{1,0:T(8,128)S(1)} %copy-done.3, bf16[512,256]{1,0:T(8,128)(2,1)S(1)} %copy-done.1, bf16[512,256]{1,0:T(8,128)(2,1)S(1)} %copy-done, f32[16,8,216,128]{3,2,1,0:T(8,128)S(1)} %bitcast.6), custom_call_target="tpu_custom_call" | custom-call | tf_op jit(solution)/shard_map/middle/pallas_call | solution.py:265
  196.4 68.8 %all_to_all.11.in_ref = f32[128,80,128]{2,1,0:T(8,128)S(1)} all-to-all(f32[128,80,128]{2,1,0:T(8,128)S(1)} %bitcast.7), channel_id=1, replica_groups=mesh['row'=8,'col'=16] {'col','row'}, dimensions={0} | all-to-all | bytes 10485760 | tf_op jit(solution)/shard_map/all_to_all | solution.py:361
  265.3 3.4 %unpack.1 = (f32[4,512,512]{2,1,0:T(8,128)}, f32[512,512]{1,0:T(8,128)}) custom-call(f32[128,80,128]{2,1,0:T(8,128)S(1)} %all_to_all.11.in_ref), custom_call_target="tpu_custom_call" | custom-call | tf_op jit(solution)/shard_map/unpack/pallas_call | solution.py:339
Async XLA Ops:
  9.3 171.8 %copy-start = (bf16[512,256]{1,0:T(8,128)(2,1)S(1)}, bf16[512,256]{1,0:T(8,128)(2,1)}, u32[]{:S(2)}) copy-start(bf16[512,256]{1,0:T(8,128)(2,1)} %constant.5.clone.low_ref) | copy-start | bytes 786436
  9.3 171.8 %copy-start.1 = (bf16[512,256]{1,0:T(8,128)(2,1)S(1)}, bf16[512,256]{1,0:T(8,128)(2,1)}, u32[]{:S(2)}) copy-start(bf16[512,256]{1,0:T(8,128)(2,1)} %constant.4.clone.high_ref) | copy-start | bytes 786436
  9.3 171.8 %copy-start.2 = (s32[16,16]{1,0:T(8,128)S(1)}, s32[16,16]{1,0:T(8,128)}, u32[]{:S(2)}) copy-start(s32[16,16]{1,0:T(8,128)} %places.1) | copy-start | bytes 3076
  9.4 171.8 %copy-start.3 = (s32[16,16]{1,0:T(8,128)S(1)}, s32[16,16]{1,0:T(8,128)}, u32[]{:S(2)}) copy-start(s32[16,16]{1,0:T(8,128)} %columns.1) | copy-start | bytes 3076
  9.4 171.8 %copy-start.4 = (s32[16]{0:T(128)S(1)}, s32[16]{0:T(128)}, u32[]{:S(2)}) copy-start(s32[16]{0:T(128)} %sizes.1) | copy-start | bytes 196

commit v6 on v5

--- a/solution.py
+++ b/solution.py
@@ -15,7 +15,7 @@
 ROWS = 72
 CAP = 36
 SENT = 3 * ROWS
-PLACED = 80
+PLACED = 72
 ZB = 32
 NB = 16
 NR = 8
@@ -249,8 +249,10 @@
 
     lax.fori_loop(0, 4, one, 0)
     peak = jnp.max(top[...].reshape(16, 8, LANES), axis=1)
-    spread[...] = jnp.broadcast_to(peak[None, None], spread.shape)
-    last = pltpu.make_async_copy(spread, out_ref.at[:, :, pl.ds(64, 16), :], peak_sem)
+    for column in range(NB):
+        half = peak[:8] if column % 2 == 0 else peak[8:]
+        spread[column] = jnp.broadcast_to(half[None], (NR, 8, LANES))
+    last = pltpu.make_async_copy(spread, out_ref.at[:, :, pl.ds(64, 8), :], peak_sem)
     last.start()
     for quad in range(4):
         for side in range(2):
@@ -279,7 +281,7 @@
             pltpu.VMEM((KX, N, LANES), jnp.float32),
             pltpu.VMEM((4, 32, MADE, LANES), jnp.float32),
             pltpu.VMEM((LANES, LANES), jnp.float32),
-            pltpu.VMEM((NB, NR, 16, LANES), jnp.float32),
+            pltpu.VMEM((NB, NR, 8, LANES), jnp.float32),
             pltpu.SemaphoreType.DMA((2,)),
             pltpu.SemaphoreType.DMA((4, 2)),
             pltpu.SemaphoreType.DMA,
@@ -289,7 +291,7 @@
     )(y_sizes, old_place, new_col, *matrices, received.reshape(NB, NR, SENT, LANES))
 
 
-def unpack_kernel(in_ref, slab_ref, peak_ref, taken, slab, peak, in_sem, slab_sem, peak_sem):
+def unpack_kernel(in_ref, slab_ref, taken, slab, in_sem, slab_sem):
     def load(t):
         return pltpu.make_async_copy(
             in_ref.at[:, pl.ds(t * 8, 8), :], taken.at[t], in_sem.at[t]
@@ -303,35 +305,18 @@
             slab_sem.at[t],
         )
 
-    def store_peak(t):
-        return pltpu.make_async_copy(
-            peak.at[t], peak_ref.at[:, pl.ds(t * 256, 256)], peak_sem.at[t]
-        )
-
-    def turn(t, row):
-        flat = taken.at[t].reshape(DEVICES * 8, LANES)
-        return flat[pl.ds(row, DEVICES, stride=8), :].T
-
-    for t in range(10):
+    for t in range(8):
         load(t).start()
     for t in range(8):
         load(t).wait()
+        flat = taken.at[t].reshape(DEVICES * 8, LANES)
         for j in range(2):
             for gp in range(4):
-                slab[t, gp, j * LANES : (j + 1) * LANES, :] = turn(t, j * 4 + gp)
+                tile = flat[pl.ds(j * 4 + gp, DEVICES, stride=8), :].T
+                slab[t, gp, j * LANES : (j + 1) * LANES, :] = tile
         store(t).start()
-    for t in range(2):
-        load(8 + t).wait()
-        for half in range(2):
-            for yb in range(4):
-                peak[t, yb * LANES : (yb + 1) * LANES, half * LANES : (half + 1) * LANES] = turn(
-                    8 + t, half * 4 + yb
-                )
-        store_peak(t).start()
     for t in range(8):
         store(t).wait()
-    for t in range(2):
-        store_peak(t).wait()
 
 
 def unpack(arrived):
@@ -339,22 +324,65 @@
     return pl.pallas_call(
         unpack_kernel,
         in_specs=[anywhere],
-        out_specs=[anywhere, anywhere],
-        out_shape=[
-            jax.ShapeDtypeStruct((4, N, N), jnp.float32),
-            jax.ShapeDtypeStruct((N, N), jnp.float32),
-        ],
+        out_specs=anywhere,
+        out_shape=jax.ShapeDtypeStruct((4, N, N), jnp.float32),
         scratch_shapes=[
-            pltpu.VMEM((10, DEVICES, 8, LANES), jnp.float32),
+            pltpu.VMEM((8, DEVICES, 8, LANES), jnp.float32),
             pltpu.VMEM((8, 4, 256, LANES), jnp.float32),
-            pltpu.VMEM((2, N, 256), jnp.float32),
-            pltpu.SemaphoreType.DMA((10,)),
             pltpu.SemaphoreType.DMA((8,)),
-            pltpu.SemaphoreType.DMA((2,)),
+            pltpu.SemaphoreType.DMA((8,)),
         ],
         name="unpack",
-        compiler_params=pltpu.CompilerParams(vmem_limit_bytes=16 << 20),
+        compiler_params=pltpu.CompilerParams(vmem_limit_bytes=60 << 20),
+        cost_estimate=pl.CostEstimate(
+            flops=N * N * N * 16, bytes_accessed=32 * N * N, transcendentals=0
+        ),
     )(arrived)
+
+
+def unpack_half_kernel(in_ref, out_ref):
+    flat = in_ref.reshape(DEVICES * 8, LANES)
+    for k in range(2):
+        for yb in range(4):
+            tile = flat[pl.ds(k * 4 + yb, DEVICES, stride=8), :].T
+            out_ref[yb * LANES : (yb + 1) * LANES, k * LANES : (k + 1) * LANES] = tile
+
+
+def unpack_half(arrived):
+    return pl.pallas_call(
+        unpack_half_kernel,
+        grid=(1,),
+        in_specs=[pl.BlockSpec((DEVICES, 8, LANES), lambda i: (0, 8, 0))],
+        out_specs=pl.BlockSpec((N, HALF), lambda i: (0, 0)),
+        out_shape=jax.ShapeDtypeStruct((N, HALF), jnp.float32),
+        name="unpack_half",
+        compiler_params=pltpu.CompilerParams(vmem_limit_bytes=60 << 20),
+    )(arrived)
+
+
+def join_kernel(core, mine_ref, other_ref, out_ref, sem):
+    at = pl.multiple_of(core[0] * HALF, HALF)
+    copies = (
+        pltpu.make_async_copy(mine_ref, out_ref.at[:, pl.ds(at, HALF)], sem.at[0]),
+        pltpu.make_async_copy(other_ref, out_ref.at[:, pl.ds(HALF - at, HALF)], sem.at[1]),
+    )
+    for copy in copies:
+        copy.start()
+    for copy in copies:
+        copy.wait()
+
+
+def join(mine, other, core):
+    anywhere = pl.BlockSpec(memory_space=pl.ANY)
+    return pl.pallas_call(
+        join_kernel,
+        in_specs=[pl.BlockSpec(memory_space=pltpu.SMEM), anywhere, anywhere],
+        out_specs=anywhere,
+        out_shape=jax.ShapeDtypeStruct((N, N), jnp.float32),
+        scratch_shapes=[pltpu.SemaphoreType.DMA((2,))],
+        name="join",
+        compiler_params=pltpu.CompilerParams(vmem_limit_bytes=60 << 20),
+    )(core, mine, other)
 
 
 def exchange(value):
@@ -365,7 +393,12 @@
     matrices = tuple(jnp.asarray(part) for part in spectral_pair())
     received = exchange(pack(velocity.reshape(3, ROWS, ZB, N), matrices))
     packed = middle(received, matrices, y_sizes, old_place, new_col)
-    slab, peak = unpack(exchange(packed.reshape(DEVICES, PLACED, LANES)))
+    arrived = exchange(packed.reshape(DEVICES, PLACED, LANES))
+    mine = unpack_half(arrived)
+    other = lax.ppermute(mine, "col", [(c, c ^ 1) for c in range(lax.axis_size("col"))])
+    slab = unpack(arrived)
+    core = lax.axis_index("col") & 1
+    peak = join(mine, other, jnp.full((1,), core, jnp.int32))
     return slab.reshape(2, 1, 2, N, N), peak
 
 

time: 269 us -> 301 us (1.12)
  Pallas kernels: 27.3 us -> 62.4 us
  blocking collectives: 241 us -> 235 us
    pallas_call x1 -> x3, Pallas kernels: 3.38 us -> 38.5 us  [the longest x1 32.9 us: join(): pl.pallas_call(join_kernel, in_specs=[pl.BlockSpec(memory_space=pltpu.SME...]
    all_to_all x2, blocking collectives: 241 us -> 235 us  [exchange(): return lax.all_to_all(value, AXES, split_axis=0, concat_axis=0, tiled=True)]
  transfers between devices with their start and end apart: 0 -> 1, of which waited for: 0 -> 0; matrix products, arithmetic and copies ran while one was open for 0% -> 0% of each run, Pallas kernels for 0% -> 1%
where the time goes in v6:
time: 301 us; the launch traced here: 299 us
  blocking collectives  235 us (78%)
  Pallas kernels  62.4 us (21%)
    all_to_all x2, blocking collectives, exchange(): return lax.all_to_all(value, AXES, split_axis=0, concat_axis=0, tiled=True)  235 us
    pallas_call x1, Pallas kernels, join(): pl.pallas_call(join_kernel, in_specs=[pl.BlockSpec(memory_space=pltpu.SME...  32.9 us
    pallas_call x1, Pallas kernels, middle(): pl.pallas_call(middle_kernel, in_specs=[near, near, near, far, far, pl.Bl...  15.2 us
    pallas_call x1, Pallas kernels, pack(): pl.pallas_call(pack_kernel, in_specs=[far, far, far], out_specs=pl.BlockS...  8.69 us
  transfers between devices with their start and end apart: 1, of which 0 were waited for; matrix products, arithmetic and copies ran while one was open for 0% of the time, Pallas kernels for 1%

profile of v6, /device:TPU:0, one launch (start us, length us, event | category | flops | bytes accessed | tf_op | source)
XLA Modules:
  0.0 299.0 jit_solution(3494811806408410987)
XLA Ops:
  0.6 8.7 %pack.1 = f32[128,216,128]{2,1,0:T(8,128)S(1)} custom-call(f32[3,72,32,512]{3,2,1,0:T(8,128)} %bitcast.9, bf16[512,256]{1,0:T(8,128)(2,1)} %constant.10.clone.high_ref, bf16[512,256]{1,0:T(8,128)(2,1)} %constant.11.clone.low_ref), custom_call_target="tpu_custom_call" | custom-call | tf_op jit(solution)/shard_map/pack/pallas_call | solution.py:117
  9.3 0.0 copy-start
  9.3 0.0 copy-start.1
  9.3 0.0 copy-start.2
  9.4 0.0 copy-start.3
  9.4 0.0 copy-start.4
  9.4 171.8 %all_to_all.10 = f32[128,216,128]{2,1,0:T(8,128)S(1)} all-to-all(f32[128,216,128]{2,1,0:T(8,128)S(1)} %pack.1), channel_id=1, replica_groups=mesh['row'=8,'col'=16] {'col','row'}, dimensions={0} | all-to-all | bytes 28311552 | tf_op jit(solution)/shard_map/all_to_all | solution.py:389
  181.1 0.0 copy-done
  181.1 0.0 copy-done.1
  181.1 0.0 copy-done.2
  181.2 0.0 copy-done.3
  181.2 0.0 copy-done.4
  181.2 15.2 %middle.1 = f32[16,8,72,128]{3,2,1,0:T(8,128)S(1)} custom-call(s32[16]{0:T(128)S(1)} %copy-done.4, s32[16,16]{1,0:T(8,128)S(1)} %copy-done.2, s32[16,16]{1,0:T(8,128)S(1)} %copy-done.3, bf16[512,256]{1,0:T(8,128)(2,1)S(1)} %copy-done, bf16[512,256]{1,0:T(8,128)(2,1)S(1)} %copy-done.1, f32[16,8,216,128]{3,2,1,0:T(8,128)S(1)} %bitcast.7), custom_call_target="tpu_custom_call" | custom-call | tf_op jit(solution)/shard_map/middle/pallas_call | solution.py:267
  196.4 63.3 %all_to_all.11.in_ref = f32[128,72,128]{2,1,0:T(8,128)} all-to-all(f32[128,72,128]{2,1,0:T(8,128)S(1)} %bitcast.8), channel_id=1, replica_groups=mesh['row'=8,'col'=16] {'col','row'}, dimensions={0} | all-to-all | bytes 9437184 | tf_op jit(solution)/shard_map/all_to_all | solution.py:389
  259.6 2.0 unpack_half.1.mine_ref
  261.7 0.0 collective-permute-start
  261.7 3.6 %unpack.1 = f32[4,512,512]{2,1,0:T(8,128)} custom-call(f32[128,72,128]{2,1,0:T(8,128)} %all_to_all.11.in_ref), custom_call_target="tpu_custom_call" | custom-call | flops 2147483648 | bytes 8388608 | tf_op jit(solution)/shard_map/unpack/pallas_call | solution.py:324
  265.3 0.0 collective-permute-done.other_ref
  265.3 0.0 copy-start.5
  265.3 0.8 copy-done.5
  266.1 32.9 %join.1 = f32[512,512]{1,0:T(8,128)} custom-call(s32[1]{0:T(128)} %bitcast.5.core, f32[512,256]{1,0:T(8,128)} %unpack_half.1.mine_ref, f32[512,256]{1,0:T(8,128)} %copy-done.5), custom_call_target="tpu_custom_call" | custom-call | tf_op jit(solution)/shard_map/join/pallas_call | solution.py:377
Async XLA Ops:
  9.3 171.8 %copy-start = (bf16[512,256]{1,0:T(8,128)(2,1)S(1)}, bf16[512,256]{1,0:T(8,128)(2,1)}, u32[]{:S(2)}) copy-start(bf16[512,256]{1,0:T(8,128)(2,1)} %constant.10.clone.high_ref) | copy-start | bytes 786436
  9.3 171.8 %copy-start.1 = (bf16[512,256]{1,0:T(8,128)(2,1)S(1)}, bf16[512,256]{1,0:T(8,128)(2,1)}, u32[]{:S(2)}) copy-start(bf16[512,256]{1,0:T(8,128)(2,1)} %constant.11.clone.low_ref) | copy-start | bytes 786436
  9.3 171.8 %copy-start.2 = (s32[16,16]{1,0:T(8,128)S(1)}, s32[16,16]{1,0:T(8,128)}, u32[]{:S(2)}) copy-start(s32[16,16]{1,0:T(8,128)} %places.1) | copy-start | bytes 3076
  9.4 171.8 %copy-start.3 = (s32[16,16]{1,0:T(8,128)S(1)}, s32[16,16]{1,0:T(8,128)}, u32[]{:S(2)}) copy-start(s32[16,16]{1,0:T(8,128)} %columns.1) | copy-start | bytes 3076
  9.4 171.8 %copy-start.4 = (s32[16]{0:T(128)S(1)}, s32[16]{0:T(128)}, u32[]{:S(2)}) copy-start(s32[16]{0:T(128)} %sizes.1) | copy-start | bytes 196
  261.7 3.6 %collective-permute-start = (f32[512,256]{1,0:T(8,128)}, f32[512,256]{1,0:T(8,128)S(1)}, u32[]{:S(2)}, u32[]{:S(2)}) collective-permute-start(f32[512,256]{1,0:T(8,128)} %unpack_half.1.mine_ref), channel_id=1, source_target_pairs={{0,1},{1,0},{2,3},{3,2},{4,5},{5,4},{6,7},{7,6},{8,9},{9,8},{10,11... | collective-permute-start | bytes 1572872 | tf_op jit(solution)/shard_map/ppermute | solution.py:398
  265.3 0.8 copy-start.5

commit v7 on v5

--- a/solution.py
+++ b/solution.py
@@ -154,7 +154,7 @@
 
 def middle_kernel(
     sizes, places, columns, high_ref, low_ref, in_ref, out_ref,
-    starts, first, high, low, lined, field, part, slope_y, total, made, top, spread,
+    starts, first, high, low, lined, second, part, slope_y, total, shared, top, spread,
     sem, out_sem, peak_sem,
 ):
     constants = (
@@ -177,8 +177,12 @@
 
     lax.fori_loop(0, NB, rows_of, 0)
     flat = in_ref.reshape(NB, NR * SENT, LANES)
-
-    def line_up(item, quad):
+    made = shared.reshape(4, 32, MADE, LANES)
+
+    def field_rows(k, quad):
+        return pl.ds(pl.multiple_of((k * 4 + quad) * N, N), N)
+
+    def line_up(item, quad, lined=lined):
         for cc in range(4):
             for b in range(NB):
                 row = first[quad * 4 + cc, b] + item * ROWS
@@ -195,18 +199,27 @@
         line_up(0, quad)
         turned = turn_lanes([lined[cc, 0:N, :] for cc in range(4)])
         for k in range(KX):
-            field[k, quad] = turned[k]
+            shared[field_rows(k, quad), :] = turned[k]
+        line_up(1, quad, second)
+        wide = jnp.concatenate([second[cc, 0:N, :] for cc in range(4)], axis=1)
+        slope = derive_rows(wide, high[...], low[...])
+        for cc in range(4):
+            slope_y[quad, cc] = slope[:, cc * LANES : (cc + 1) * LANES]
         return carry
 
-    lax.fori_loop(0, 4, split_z, 0)
     for copy in constants:
         copy.wait()
+    lax.fori_loop(0, 4, split_z, 0)
 
     def slope_z(k, carry):
-        line = jnp.concatenate([field[k, quad] for quad in range(4)], axis=1)
+        line = jnp.concatenate([shared[field_rows(k, quad), :] for quad in range(4)], axis=1)
         slope = derive_lanes(line, high[...], low[...])
         for quad in range(4):
             part[quad, k] = slope[:, quad * LANES : (quad + 1) * LANES]
+        line_up(2, k)
+        turned = turn_lanes([slope_y[k, cc] + lined[cc, 0:N, :] for cc in range(4)])
+        for cc in range(4):
+            slope_y[k, cc] = turned[cc]
         return carry
 
     lax.fori_loop(0, KX, slope_z, 0)
@@ -216,23 +229,16 @@
     lane_column = lane % NB
 
     def one(quad, carry):
-        line_up(1, quad)
-        wide = jnp.concatenate([lined[cc, 0:N, :] for cc in range(4)], axis=1)
-        slope = derive_rows(wide, high[...], low[...])
-        for cc in range(4):
-            slope_y[cc] = slope[:, cc * LANES : (cc + 1) * LANES]
         order = lane_block * ZB + (lane // 32) % 2
         for cc in range(4):
             for slab in range(NB):
                 hit = (lane_block == cc) & (lane_column == columns[quad * 4 + cc, slab])
                 order = order + jnp.where(hit, 2 * slab, 0)
         order = jnp.concatenate([order] * (CHUNK // 8), axis=0)
-        line_up(2, quad)
         for at in range(0, N, CHUNK):
             rows = slice(at, at + CHUNK)
-            turned = turn_lanes([slope_y[cc, rows, :] + lined[cc, rows, :] for cc in range(4)])
             for k in range(KX):
-                value = turned[k] + part[quad, k, rows, :]
+                value = slope_y[quad, k, rows, :] + part[quad, k, rows, :]
                 total[k, rows, :] = jnp.take_along_axis(value, order, axis=1)
         for k in range(KX):
             for yb in range(4):
@@ -273,11 +279,11 @@
             pltpu.VMEM((N, HALF), jnp.bfloat16),
             pltpu.VMEM((N, HALF), jnp.bfloat16),
             pltpu.VMEM((4, LINED, LANES), jnp.float32),
-            pltpu.VMEM((KX, 4, N, LANES), jnp.float32),
+            pltpu.VMEM((4, LINED, LANES), jnp.float32),
             pltpu.VMEM((4, KX, N, LANES), jnp.float32),
-            pltpu.VMEM((4, N, LANES), jnp.float32),
+            pltpu.VMEM((4, 4, N, LANES), jnp.float32),
             pltpu.VMEM((KX, N, LANES), jnp.float32),
-            pltpu.VMEM((4, 32, MADE, LANES), jnp.float32),
+            pltpu.VMEM((4 * 32 * MADE, LANES), jnp.float32),
             pltpu.VMEM((LANES, LANES), jnp.float32),
             pltpu.VMEM((NB, NR, 16, LANES), jnp.float32),
             pltpu.SemaphoreType.DMA((2,)),

time: 269 us -> 266 us (0.989)
  Pallas kernels: 27.3 us -> 24 us
    pallas_call x1, Pallas kernels: 15.3 us -> 11.9 us  [middle(): pl.pallas_call(middle_kernel, in_specs=[near, near, near, far, far, pl.Bl...]
where the time goes in v7:
time: 266 us
  blocking collectives  241 us (91%)
  Pallas kernels  24 us (9%)
    all_to_all x2, blocking collectives, exchange(): return lax.all_to_all(value, AXES, split_axis=0, concat_axis=0, tiled=True)  241 us
    pallas_call x1, Pallas kernels, middle(): pl.pallas_call(middle_kernel, in_specs=[near, near, near, far, far, pl.Bl...  11.9 us
    pallas_call x1, Pallas kernels, pack(): pl.pallas_call(pack_kernel, in_specs=[far, far, far], out_specs=pl.BlockS...  8.68 us

profile of v7, /device:TPU:0, one launch (start us, length us, event | category | flops | bytes accessed | tf_op | source)
XLA Modules:
  0.0 265.5 jit_solution(15576759576616743880)
XLA Ops:
  0.6 8.7 %pack.1 = f32[128,216,128]{2,1,0:T(8,128)S(1)} custom-call(f32[3,72,32,512]{3,2,1,0:T(8,128)} %bitcast.8, bf16[512,256]{1,0:T(8,128)(2,1)} %constant.4.clone.high_ref, bf16[512,256]{1,0:T(8,128)(2,1)} %constant.5.clone.low_ref), custom_call_target="tpu_custom_call" | custom-call | tf_op jit(solution)/shard_map/pack/pallas_call | solution.py:117
  9.3 0.0 copy-start
  9.3 0.0 copy-start.1
  9.3 0.0 copy-start.2
  9.4 0.0 copy-start.3
  9.4 0.0 copy-start.4
  9.4 171.8 %all_to_all.10 = f32[128,216,128]{2,1,0:T(8,128)S(1)} all-to-all(f32[128,216,128]{2,1,0:T(8,128)S(1)} %pack.1), channel_id=1, replica_groups=mesh['row'=8,'col'=16] {'col','row'}, dimensions={0} | all-to-all | bytes 28311552 | tf_op jit(solution)/shard_map/all_to_all | solution.py:367
  181.1 0.0 copy-done
  181.2 0.0 copy-done.1
  181.2 0.0 copy-done.2
  181.2 0.0 copy-done.3
  181.2 0.0 copy-done.4
  181.2 11.9 %middle.1 = f32[16,8,80,128]{3,2,1,0:T(8,128)S(1)} custom-call(s32[16]{0:T(128)S(1)} %copy-done.4, s32[16,16]{1,0:T(8,128)S(1)} %copy-done.2, s32[16,16]{1,0:T(8,128)S(1)} %copy-done.3, bf16[512,256]{1,0:T(8,128)(2,1)S(1)} %copy-done.1, bf16[512,256]{1,0:T(8,128)(2,1)S(1)} %copy-done, f32[16,8,216,128]{3,2,1,0:T(8,128)S(1)} %bitcast.6), custom_call_target="tpu_custom_call" | custom-call | tf_op jit(solution)/shard_map/middle/pallas_call | solution.py:271
  193.1 68.8 %all_to_all.11.in_ref = f32[128,80,128]{2,1,0:T(8,128)S(1)} all-to-all(f32[128,80,128]{2,1,0:T(8,128)S(1)} %bitcast.7), channel_id=1, replica_groups=mesh['row'=8,'col'=16] {'col','row'}, dimensions={0} | all-to-all | bytes 10485760 | tf_op jit(solution)/shard_map/all_to_all | solution.py:367
  262.0 3.4 %unpack.1 = (f32[4,512,512]{2,1,0:T(8,128)}, f32[512,512]{1,0:T(8,128)}) custom-call(f32[128,80,128]{2,1,0:T(8,128)S(1)} %all_to_all.11.in_ref), custom_call_target="tpu_custom_call" | custom-call | tf_op jit(solution)/shard_map/unpack/pallas_call | solution.py:345
Async XLA Ops:
  9.3 171.8 %copy-start = (bf16[512,256]{1,0:T(8,128)(2,1)S(1)}, bf16[512,256]{1,0:T(8,128)(2,1)}, u32[]{:S(2)}) copy-start(bf16[512,256]{1,0:T(8,128)(2,1)} %constant.5.clone.low_ref) | copy-start | bytes 786436
  9.3 171.8 %copy-start.1 = (bf16[512,256]{1,0:T(8,128)(2,1)S(1)}, bf16[512,256]{1,0:T(8,128)(2,1)}, u32[]{:S(2)}) copy-start(bf16[512,256]{1,0:T(8,128)(2,1)} %constant.4.clone.high_ref) | copy-start | bytes 786436
  9.3 171.8 %copy-start.2 = (s32[16,16]{1,0:T(8,128)S(1)}, s32[16,16]{1,0:T(8,128)}, u32[]{:S(2)}) copy-start(s32[16,16]{1,0:T(8,128)} %places.1) | copy-start | bytes 3076
  9.4 171.8 %copy-start.3 = (s32[16,16]{1,0:T(8,128)S(1)}, s32[16,16]{1,0:T(8,128)}, u32[]{:S(2)}) copy-start(s32[16,16]{1,0:T(8,128)} %columns.1) | copy-start | bytes 3076
  9.4 171.8 %copy-start.4 = (s32[16]{0:T(128)S(1)}, s32[16]{0:T(128)}, u32[]{:S(2)}) copy-start(s32[16]{0:T(128)} %sizes.1) | copy-start | bytes 196

commit v8 on v7

--- a/solution.py
+++ b/solution.py
@@ -93,23 +93,34 @@
         pltpu.make_async_copy(high_ref, high, sem.at[0]),
         pltpu.make_async_copy(low_ref, low, sem.at[1]),
     )
-    for step in range(3 * STEPS):
+    groups = [range(group, group + GROUP) for group in range(0, STEPS, GROUP)]
+    for step in range(STEPS):
         load(step).start()
     for copy in constants:
         copy.start()
-    for step in range(2 * STEPS):
+    for group in groups:
+        for item in (2, 1):
+            for step in group:
+                load(item * STEPS + step).start()
+
+    for step in range(STEPS):
         load(step).wait()
         for i in range(8):
             pack_row(taken[step, i], flat, step * 8 + i)
     for copy in constants:
         copy.wait()
-    for group in range(2 * STEPS, 3 * STEPS, GROUP):
-        for step in range(group, group + GROUP):
-            load(step).wait()
-        lines = taken[group : group + GROUP].reshape(GROUP * 8 * ZB, N)
+    for group in groups:
+        for item in (2, 1):
+            for step in group:
+                load(item * STEPS + step).wait()
+        at = 2 * STEPS + group[0]
+        lines = taken[at : at + GROUP].reshape(GROUP * 8 * ZB, N)
         slope = derive_lanes(lines, high[...], low[...])
+        for step in group:
+            for i in range(8):
+                pack_row(taken[STEPS + step, i], flat, (STEPS + step) * 8 + i)
         for i in range(GROUP * 8):
-            pack_row(slope[i * ZB : (i + 1) * ZB], flat, group * 8 + i)
+            pack_row(slope[i * ZB : (i + 1) * ZB], flat, at * 8 + i)
 
 
 def pack(velocity, matrices):
@@ -301,43 +312,41 @@
             in_ref.at[:, pl.ds(t * 8, 8), :], taken.at[t], in_sem.at[t]
         )
 
-    def store(t):
-        k, m = divmod(t, 2)
+    def store(yb):
         return pltpu.make_async_copy(
-            slab.at[t],
-            slab_ref.at[:, pl.ds(m * 256, 256), pl.ds(k * LANES, LANES)],
-            slab_sem.at[t],
-        )
-
-    def store_peak(t):
-        return pltpu.make_async_copy(
-            peak.at[t], peak_ref.at[:, pl.ds(t * 256, 256)], peak_sem.at[t]
+            slab.at[yb], slab_ref.at[:, pl.ds(yb * LANES, LANES), :], slab_sem.at[yb]
         )
 
     def turn(t, row):
         flat = taken.at[t].reshape(DEVICES * 8, LANES)
         return flat[pl.ds(row, DEVICES, stride=8), :].T
 
-    for t in range(10):
-        load(t).start()
-    for t in range(8):
-        load(t).wait()
+    for m in range(2):
+        for k in range(KX):
+            load(k * 2 + m).start()
+    for t in range(2):
+        load(8 + t).start()
+    for m in range(2):
+        for k in range(KX):
+            load(k * 2 + m).wait()
         for j in range(2):
+            yb = m * 2 + j
             for gp in range(4):
-                slab[t, gp, j * LANES : (j + 1) * LANES, :] = turn(t, j * 4 + gp)
-        store(t).start()
+                for k in range(KX):
+                    slab[yb, gp, :, k * LANES : (k + 1) * LANES] = turn(k * 2 + m, j * 4 + gp)
+            store(yb).start()
     for t in range(2):
         load(8 + t).wait()
         for half in range(2):
             for yb in range(4):
-                peak[t, yb * LANES : (yb + 1) * LANES, half * LANES : (half + 1) * LANES] = turn(
-                    8 + t, half * 4 + yb
-                )
-        store_peak(t).start()
-    for t in range(8):
-        store(t).wait()
-    for t in range(2):
-        store_peak(t).wait()
+                k = t * 2 + half
+                rows = slice(yb * LANES, (yb + 1) * LANES)
+                peak[rows, k * LANES : (k + 1) * LANES] = turn(8 + t, half * 4 + yb)
+    last = pltpu.make_async_copy(peak, peak_ref, peak_sem)
+    last.start()
+    for yb in range(4):
+        store(yb).wait()
+    last.wait()
 
 
 def unpack(arrived):
@@ -352,11 +361,11 @@
         ],
         scratch_shapes=[
             pltpu.VMEM((10, DEVICES, 8, LANES), jnp.float32),
-            pltpu.VMEM((8, 4, 256, LANES), jnp.float32),
-            pltpu.VMEM((2, N, 256), jnp.float32),
+            pltpu.VMEM((4, 4, LANES, N), jnp.float32),
+            pltpu.VMEM((N, N), jnp.float32),
             pltpu.SemaphoreType.DMA((10,)),
-            pltpu.SemaphoreType.DMA((8,)),
-            pltpu.SemaphoreType.DMA((2,)),
+            pltpu.SemaphoreType.DMA((4,)),
+            pltpu.SemaphoreType.DMA,
         ],
         name="unpack",
         compiler_params=pltpu.CompilerParams(vmem_limit_bytes=16 << 20),

time: 266 us -> 265 us (level)
  no operation moved by 1% of the time
where the time goes in v8:
time: 265 us
  blocking collectives  241 us (91%)
  Pallas kernels  23.7 us (9%)
    all_to_all x2, blocking collectives, exchange(): return lax.all_to_all(value, AXES, split_axis=0, concat_axis=0, tiled=True)  241 us
    pallas_call x1, Pallas kernels, middle(): pl.pallas_call(middle_kernel, in_specs=[near, near, near, far, far, pl.Bl...  11.9 us
    pallas_call x1, Pallas kernels, pack(): pl.pallas_call(pack_kernel, in_specs=[far, far, far], out_specs=pl.BlockS...  8.63 us

profile of v8, /device:TPU:0, one launch (start us, length us, event | category | flops | bytes accessed | tf_op | source)
XLA Modules:
  0.0 265.1 jit_solution(221164496792232072)
XLA Ops:
  0.6 8.6 %pack.1 = f32[128,216,128]{2,1,0:T(8,128)S(1)} custom-call(f32[3,72,32,512]{3,2,1,0:T(8,128)} %bitcast.8, bf16[512,256]{1,0:T(8,128)(2,1)} %constant.4.clone.high_ref, bf16[512,256]{1,0:T(8,128)(2,1)} %constant.5.clone.low_ref), custom_call_target="tpu_custom_call" | custom-call | tf_op jit(solution)/shard_map/pack/pallas_call | solution.py:128
  9.3 0.0 copy-start
  9.3 0.0 copy-start.1
  9.3 0.0 copy-start.2
  9.3 0.0 copy-start.3
  9.3 0.0 copy-start.4
  9.3 171.8 %all_to_all.10 = f32[128,216,128]{2,1,0:T(8,128)S(1)} all-to-all(f32[128,216,128]{2,1,0:T(8,128)S(1)} %pack.1), channel_id=1, replica_groups=mesh['row'=8,'col'=16] {'col','row'}, dimensions={0} | all-to-all | bytes 28311552 | tf_op jit(solution)/shard_map/all_to_all | solution.py:376
  181.1 0.0 copy-done
  181.1 0.0 copy-done.1
  181.1 0.0 copy-done.2
  181.1 0.0 copy-done.3
  181.1 0.0 copy-done.4
  181.1 11.9 %middle.1 = f32[16,8,80,128]{3,2,1,0:T(8,128)S(1)} custom-call(s32[16]{0:T(128)S(1)} %copy-done.4, s32[16,16]{1,0:T(8,128)S(1)} %copy-done.2, s32[16,16]{1,0:T(8,128)S(1)} %copy-done.3, bf16[512,256]{1,0:T(8,128)(2,1)S(1)} %copy-done.1, bf16[512,256]{1,0:T(8,128)(2,1)S(1)} %copy-done, f32[16,8,216,128]{3,2,1,0:T(8,128)S(1)} %bitcast.6), custom_call_target="tpu_custom_call" | custom-call | tf_op jit(solution)/shard_map/middle/pallas_call | solution.py:282
  193.1 68.8 %all_to_all.11.in_ref = f32[128,80,128]{2,1,0:T(8,128)S(1)} all-to-all(f32[128,80,128]{2,1,0:T(8,128)S(1)} %bitcast.7), channel_id=1, replica_groups=mesh['row'=8,'col'=16] {'col','row'}, dimensions={0} | all-to-all | bytes 10485760 | tf_op jit(solution)/shard_map/all_to_all | solution.py:376
  261.9 3.2 %unpack.1 = (f32[4,512,512]{2,1,0:T(8,128)}, f32[512,512]{1,0:T(8,128)}) custom-call(f32[128,80,128]{2,1,0:T(8,128)S(1)} %all_to_all.11.in_ref), custom_call_target="tpu_custom_call" | custom-call | tf_op jit(solution)/shard_map/unpack/pallas_call | solution.py:354
Async XLA Ops:
  9.3 171.8 %copy-start = (bf16[512,256]{1,0:T(8,128)(2,1)S(1)}, bf16[512,256]{1,0:T(8,128)(2,1)}, u32[]{:S(2)}) copy-start(bf16[512,256]{1,0:T(8,128)(2,1)} %constant.5.clone.low_ref) | copy-start | bytes 786436
  9.3 171.8 %copy-start.1 = (bf16[512,256]{1,0:T(8,128)(2,1)S(1)}, bf16[512,256]{1,0:T(8,128)(2,1)}, u32[]{:S(2)}) copy-start(bf16[512,256]{1,0:T(8,128)(2,1)} %constant.4.clone.high_ref) | copy-start | bytes 786436
  9.3 171.8 %copy-start.2 = (s32[16,16]{1,0:T(8,128)S(1)}, s32[16,16]{1,0:T(8,128)}, u32[]{:S(2)}) copy-start(s32[16,16]{1,0:T(8,128)} %places.1) | copy-start | bytes 3076
  9.3 171.8 %copy-start.3 = (s32[16,16]{1,0:T(8,128)S(1)}, s32[16,16]{1,0:T(8,128)}, u32[]{:S(2)}) copy-start(s32[16,16]{1,0:T(8,128)} %columns.1) | copy-start | bytes 3076
  9.3 171.8 %copy-start.4 = (s32[16]{0:T(128)S(1)}, s32[16]{0:T(128)}, u32[]{:S(2)}) copy-start(s32[16]{0:T(128)} %sizes.1) | copy-start | bytes 196

commit v9 on v8

--- a/solution.py
+++ b/solution.py
@@ -264,7 +264,7 @@
             store(quad, side).start()
         return carry
 
-    lax.fori_loop(0, 4, one, 0)
+    lax.fori_loop(0, 4, one, 0, unroll=2)
     peak = jnp.max(top[...].reshape(16, 8, LANES), axis=1)
     spread[...] = jnp.broadcast_to(peak[None, None], spread.shape)
     last = pltpu.make_async_copy(spread, out_ref.at[:, :, pl.ds(64, 16), :], peak_sem)

time: 265 us -> 265 us (level)
  no operation moved by 1% of the time
where the time goes in v9:
time: 265 us
  blocking collectives  241 us (91%)
  Pallas kernels  23.7 us (9%)
    all_to_all x2, blocking collectives, exchange(): return lax.all_to_all(value, AXES, split_axis=0, concat_axis=0, tiled=True)  241 us
    pallas_call x1, Pallas kernels, middle(): pl.pallas_call(middle_kernel, in_specs=[near, near, near, far, far, pl.Bl...  11.9 us
    pallas_call x1, Pallas kernels, pack(): pl.pallas_call(pack_kernel, in_specs=[far, far, far], out_specs=pl.BlockS...  8.63 us

profile of v9, /device:TPU:0, one launch (start us, length us, event | category | flops | bytes accessed | tf_op | source)
XLA Modules:
  0.0 265.1 jit_solution(6621981423965225650)
XLA Ops:
  0.6 8.6 %pack.1 = f32[128,216,128]{2,1,0:T(8,128)S(1)} custom-call(f32[3,72,32,512]{3,2,1,0:T(8,128)} %bitcast.8, bf16[512,256]{1,0:T(8,128)(2,1)} %constant.4.clone.high_ref, bf16[512,256]{1,0:T(8,128)(2,1)} %constant.5.clone.low_ref), custom_call_target="tpu_custom_call" | custom-call | tf_op jit(solution)/shard_map/pack/pallas_call | solution.py:128
  9.3 0.0 copy-start
  9.3 0.0 copy-start.1
  9.3 0.0 copy-start.2
  9.3 0.0 copy-start.3
  9.3 0.0 copy-start.4
  9.3 171.8 %all_to_all.10 = f32[128,216,128]{2,1,0:T(8,128)S(1)} all-to-all(f32[128,216,128]{2,1,0:T(8,128)S(1)} %pack.1), channel_id=1, replica_groups=mesh['row'=8,'col'=16] {'col','row'}, dimensions={0} | all-to-all | bytes 28311552 | tf_op jit(solution)/shard_map/all_to_all | solution.py:376
  181.1 0.0 copy-done
  181.1 0.0 copy-done.1
  181.1 0.0 copy-done.2
  181.1 0.0 copy-done.3
  181.1 0.0 copy-done.4
  181.1 11.9 %middle.1 = f32[16,8,80,128]{3,2,1,0:T(8,128)S(1)} custom-call(s32[16]{0:T(128)S(1)} %copy-done.4, s32[16,16]{1,0:T(8,128)S(1)} %copy-done.2, s32[16,16]{1,0:T(8,128)S(1)} %copy-done.3, bf16[512,256]{1,0:T(8,128)(2,1)S(1)} %copy-done.1, bf16[512,256]{1,0:T(8,128)(2,1)S(1)} %copy-done, f32[16,8,216,128]{3,2,1,0:T(8,128)S(1)} %bitcast.6), custom_call_target="tpu_custom_call" | custom-call | tf_op jit(solution)/shard_map/middle/pallas_call | solution.py:282
  193.1 68.8 %all_to_all.11.in_ref = f32[128,80,128]{2,1,0:T(8,128)S(1)} all-to-all(f32[128,80,128]{2,1,0:T(8,128)S(1)} %bitcast.7), channel_id=1, replica_groups=mesh['row'=8,'col'=16] {'col','row'}, dimensions={0} | all-to-all | bytes 10485760 | tf_op jit(solution)/shard_map/all_to_all | solution.py:376
  261.9 3.2 %unpack.1 = (f32[4,512,512]{2,1,0:T(8,128)}, f32[512,512]{1,0:T(8,128)}) custom-call(f32[128,80,128]{2,1,0:T(8,128)S(1)} %all_to_all.11.in_ref), custom_call_target="tpu_custom_call" | custom-call | tf_op jit(solution)/shard_map/unpack/pallas_call | solution.py:354
Async XLA Ops:
  9.3 171.8 %copy-start = (bf16[512,256]{1,0:T(8,128)(2,1)S(1)}, bf16[512,256]{1,0:T(8,128)(2,1)}, u32[]{:S(2)}) copy-start(bf16[512,256]{1,0:T(8,128)(2,1)} %constant.5.clone.low_ref) | copy-start | bytes 786436
  9.3 171.8 %copy-start.1 = (bf16[512,256]{1,0:T(8,128)(2,1)S(1)}, bf16[512,256]{1,0:T(8,128)(2,1)}, u32[]{:S(2)}) copy-start(bf16[512,256]{1,0:T(8,128)(2,1)} %constant.4.clone.high_ref) | copy-start | bytes 786436
  9.3 171.8 %copy-start.2 = (s32[16,16]{1,0:T(8,128)S(1)}, s32[16,16]{1,0:T(8,128)}, u32[]{:S(2)}) copy-start(s32[16,16]{1,0:T(8,128)} %places.1) | copy-start | bytes 3076
  9.3 171.8 %copy-start.3 = (s32[16,16]{1,0:T(8,128)S(1)}, s32[16,16]{1,0:T(8,128)}, u32[]{:S(2)}) copy-start(s32[16,16]{1,0:T(8,128)} %columns.1) | copy-start | bytes 3076
  9.3 171.8 %copy-start.4 = (s32[16]{0:T(128)S(1)}, s32[16]{0:T(128)}, u32[]{:S(2)}) copy-start(s32[16]{0:T(128)} %sizes.1) | copy-start | bytes 196
